TPU v7x, 32 devices: a whole 2x2x4 slice. The times are simulated.
32 devices in a mesh: dp: 8 (over z, y), mp: 4 (over x, core).
Axes of the slice: x: 2, y: 2, z: 4, core: 2. Of those that a mesh axis runs over, the one named last changes fastest.
Arguments:
- tokens: bfloat16 [49152, 512], P('dp'), may hold values from -6 to 6
- w_uvqk: bfloat16 [512, 2048], P(None, 'mp')
- w_out: bfloat16 [512, 512], replicated, may hold values from -0.25 to 0.25
- hist_len: int32 [8, 24], P('dp'), may hold values from 64 to 256, as said below
- owner: int32 [8, 24], P('dp'), may hold values from 0 to 7, as said below
- recv_offset: int32 [8, 24], P('dp'), may hold values from 0 to 47, as said below
- block_start: int32 [8, 24], P('dp'), may hold values from 0 to 47, as said below
Outputs:
- packed_out: bfloat16 [49152, 512], P('dp', 'mp')
- user_state: bfloat16 [192, 512], P('dp', 'mp')
Inputs may be any that keep to these rules, and one draw needn't show every extreme that they name: User (d, u) has ceil(hist_len / 128) blocks, at most 2. owner[d, u] = (p(d) + r(u mod 8)) mod 8 for two permutations p, r of the indices of dp drawn from the seed: every owner receives exactly 24 users, and one device sends at most 3 users to one owner. On some owner every received user has 2 blocks. `recv_offset`: the users of one owner occupy disjoint runs of its 48 blocks, in the order of u; on some owner they fill all 48 blocks. `block_start`: the users of one device occupy disjoint runs of its 48 blocks, in the order of u.
All inputs are finite; a program needn't handle non-finite values.
Results may differ from a plain program's by a relative error of at most 0.0059.
Values may be sent and summed in bfloat16 or wider, within the bound.
No kernel may reach another device: no remote copies, remote signals or barrier semaphores. Data moves between devices by JAX's collectives and lax.ppermute only.
A program may use at most 128 MiB of HBM per device.

v0:
```python
import functools

import jax
import jax.numpy as jnp
from jax import lax
from jax.experimental import pallas as pl
from jax.experimental.pallas import tpu as pltpu
from jax.sharding import PartitionSpec as P


BLOCK = 128
MAXB = 2
HEAD = 128
WINDOW = MAXB * BLOCK
TAIL = 8
EPS = 1e-05
LIMIT = pltpu.CompilerParams(vmem_limit_bytes=24 * 1024 * 1024)


def in_vmem(value):
    return pltpu.with_memory_space_constraint(value, pltpu.VMEM)


def in_hbm(value):
    return pltpu.with_memory_space_constraint(value, pltpu.HBM)


def half_silu(half):
    return half + half * jnp.tanh(half)


def norm_scale(total, squares, width):
    average = total * (1.0 / width)
    variance = squares * (1.0 / width) - average * average
    return average, lax.rsqrt(variance + EPS)


def norm_half(widened):
    average, scale = norm_scale(
        jnp.sum(widened, 1, keepdims=True),
        jnp.sum(widened * widened, 1, keepdims=True),
        widened.shape[1],
    )
    return ((widened - average) * (0.5 * scale)).astype(jnp.bfloat16)


def attend_heads(halved, w_refs):
    row = lax.broadcasted_iota(jnp.int32, (BLOCK, BLOCK), 0)
    col = lax.broadcasted_iota(jnp.int32, (BLOCK, BLOCK), 1)
    causal = col <= row
    half_scale = 0.5 * HEAD ** (-0.5)
    values, gates = [], []
    for w_ref in w_refs:
        for head in range(w_ref.shape[1] // (4 * HEAD)):
            cols = slice(head * 4 * HEAD, (head + 1) * 4 * HEAD)
            half = jnp.dot(halved, w_ref[:, cols], preferred_element_type=jnp.float32)
            proj = half_silu(half).astype(jnp.bfloat16)
            u, v, q, k = (proj[:, i * HEAD : (i + 1) * HEAD] for i in range(4))
            raw = lax.dot_general(q, k, (((1,), (1,)), ((), ())), preferred_element_type=jnp.float32)
            weights = []
            for b in range(MAXB):
                rows = slice(b * BLOCK, (b + 1) * BLOCK)
                act = half_silu(raw[rows, : (b + 1) * BLOCK] * half_scale)
                pieces = [act[:, : b * BLOCK]] if b > 0 else []
                pieces.append(jnp.where(causal, act[:, b * BLOCK :], 0.0))
                if b + 1 < MAXB:
                    pieces.append(jnp.zeros((BLOCK, WINDOW - (b + 1) * BLOCK), jnp.float32))
                weights.append(jnp.concatenate(pieces, 1).astype(jnp.bfloat16))
            values.append(
                jnp.dot(jnp.concatenate(weights, 0), v, preferred_element_type=jnp.float32)
            )
            gates.append(u)
    return values, gates


def near_rows(base, widened, w_refs, out_refs):
    rows_ref, half_ref, value_ref, gate_ref = out_refs
    rows = pl.ds(pl.multiple_of(base * WINDOW, WINDOW), WINDOW)
    halved = norm_half(widened)
    rows_ref[rows, :] = widened.astype(rows_ref.dtype)
    half_ref[rows, :] = halved
    values, gates = attend_heads(halved, w_refs)
    value_ref[rows, :] = jnp.concatenate(values, 1)
    gate_ref[rows, :] = jnp.concatenate(gates, 1)


def near_home_kernel(near, total_slots, table_ref, *refs):
    block_refs, w_refs = refs[:MAXB], refs[MAXB : MAXB + near]
    tail_ref = refs[-1]
    slot = pl.program_id(0)
    tail_ref[pl.ds(pl.multiple_of(slot * TAIL, TAIL), TAIL), :] = tail_rows(
        table_ref[slot], table_ref[2 * total_slots + slot], tail_ref.shape[1]
    )
    widened = jnp.concatenate([ref[...] for ref in block_refs], 0).astype(jnp.float32)
    near_rows(slot, widened, w_refs, refs[MAXB + near : -1])


def near_owner_kernel(near, *refs):
    arrived_ref, w_refs = refs[0], refs[1 : 1 + near]
    tail_ref = refs[-1]
    slot = pl.program_id(0)
    first = pl.multiple_of(slot * (WINDOW + TAIL), TAIL)
    tail_ref[pl.ds(pl.multiple_of(slot * TAIL, TAIL), TAIL), :] = arrived_ref[
        pl.ds(first + WINDOW, TAIL), : tail_ref.shape[1]
    ]
    near_rows(slot, arrived_ref[pl.ds(first, WINDOW), :].astype(jnp.float32), w_refs, refs[1 + near : -1])


def far_kernel(mp, far, base, whole, *refs):
    w_refs = refs[:far]
    rows_ref, half_ref, near_value_ref, near_gate_ref, tail_ref, wp_ref = refs[far : far + 6]
    out_refs = refs[far + 6 : -2]
    state_ref, mixed_ref = refs[-2:]
    if whole:
        out_refs = [out_refs[0].at[s] for s in range(mp)]
    slot = pl.program_id(0)
    mine = lax.axis_index("mp")
    width = wp_ref.shape[0]
    rows = pl.ds(pl.multiple_of((base + slot) * WINDOW, WINDOW), WINDOW)
    tail = tail_ref[pl.ds(pl.multiple_of((base + slot) * TAIL, TAIL), TAIL), :]
    length = tail.astype(jnp.float32)[0:1, 0:1]
    values, gates = attend_heads(half_ref[rows, :], w_refs)
    value = jnp.concatenate([near_value_ref[rows, :]] + values, 1)
    gate = jnp.concatenate([near_gate_ref[rows, :]] + gates, 1)
    average, scale = norm_scale(
        jnp.sum(value, 1, keepdims=True) * (1.0 / WINDOW),
        jnp.sum(value * value, 1, keepdims=True) * (1.0 / WINDOW**2),
        width,
    )
    average, scale = average * WINDOW, scale * (1.0 / WINDOW)
    gated = ((value - average) * scale * gate.astype(jnp.float32)).astype(jnp.bfloat16)
    mixed = rows_ref[rows, :].astype(jnp.float32) + jnp.dot(
        gated, wp_ref[...], preferred_element_type=jnp.float32
    )
    live = lax.broadcasted_iota(jnp.int32, (WINDOW, 1), 0).astype(jnp.float32)
    mixed_ref[:WINDOW, :] = jnp.where(live < length, mixed, 0.0)
    final = jnp.sum(jnp.where(live == length - 1.0, mixed, 0.0), 0, keepdims=True)
    mixed_ref[WINDOW:, :] = jnp.broadcast_to(final, (TAIL, width))
    quarter = width // mp
    first = pl.multiple_of(slot * (WINDOW + TAIL), TAIL)
    for s in range(mp):
        start = pl.multiple_of((mine ^ s) * quarter, quarter)
        out_refs[s][pl.ds(first, WINDOW), :] = mixed_ref[:WINDOW, pl.ds(start, quarter)].astype(
            jnp.bfloat16
        )
        out_refs[s][pl.ds(first + WINDOW, TAIL), :] = tail
        state_ref[s, slot] = mixed_ref[WINDOW:, pl.ds(start, quarter)].astype(jnp.bfloat16)


def tail_rows(length, landing, width):
    lane = lax.broadcasted_iota(jnp.int32, (TAIL, width), 1)
    facts = jnp.where(lane == 0, length, jnp.where(lane == 1, landing, 0))
    return facts.astype(jnp.float32).astype(jnp.bfloat16)


def near_shapes(slots, width, heads, quarter):
    return [
        jax.ShapeDtypeStruct((slots * WINDOW, width), jnp.bfloat16),
        jax.ShapeDtypeStruct((slots * WINDOW, width), jnp.bfloat16),
        jax.ShapeDtypeStruct((slots * WINDOW, heads), jnp.float32),
        jax.ShapeDtypeStruct((slots * WINDOW, heads), jnp.bfloat16),
        jax.ShapeDtypeStruct((slots * TAIL, quarter), jnp.bfloat16),
    ]


def run_near_home(mp, table, tokens, shards, slots):
    heads = sum(w.shape[1] for w in shards) // 4
    width = tokens.shape[1]
    top = tokens.shape[0] // BLOCK - 1

    def block_map(b, slot, table_ref):
        return (jnp.minimum(table_ref[slots + slot] + b, top), 0)

    local = pl.BlockSpec(memory_space=pltpu.VMEM)
    outs = pl.pallas_call(
        functools.partial(near_home_kernel, len(shards), slots),
        grid_spec=pltpu.PrefetchScalarGridSpec(
            num_scalar_prefetch=1,
            grid=(slots,),
            in_specs=[
                pl.BlockSpec((BLOCK, width), functools.partial(block_map, b)) for b in range(MAXB)
            ]
            + [local] * len(shards),
            out_specs=[local] * 5,
        ),
        out_shape=near_shapes(slots, width, heads, width // mp),
        compiler_params=LIMIT,
        name="near_home",
    )(table, *([tokens] * MAXB), *shards)
    return [in_vmem(out) for out in outs]


def run_near_owner(mp, arrived, shards, slots):
    heads = sum(w.shape[1] for w in shards) // 4
    width = arrived.shape[1]
    local = pl.BlockSpec(memory_space=pltpu.VMEM)
    outs = pl.pallas_call(
        functools.partial(near_owner_kernel, len(shards)),
        grid=(slots,),
        in_specs=[local] * (1 + len(shards)),
        out_specs=[local] * 5,
        out_shape=near_shapes(slots, width, heads, width // mp),
        compiler_params=LIMIT,
        name="near_owner",
    )(in_vmem(arrived), *shards)
    return [in_vmem(out) for out in outs]


def run_far(mp, shards, near, w_perm, base, groups, whole):
    width = w_perm.shape[1]
    quarter = width // mp
    size = groups * (WINDOW + TAIL)
    local = pl.BlockSpec(memory_space=pltpu.VMEM)
    shapes = (
        [jax.ShapeDtypeStruct((mp, size, quarter), jnp.bfloat16)]
        if whole
        else [jax.ShapeDtypeStruct((size, quarter), jnp.bfloat16)] * mp
    )
    outs = pl.pallas_call(
        functools.partial(far_kernel, mp, len(shards), base, whole),
        grid=(groups,),
        in_specs=[local] * (len(shards) + 6),
        out_specs=[local] * (len(shapes) + 1),
        scratch_shapes=[pltpu.VMEM((WINDOW + TAIL, width), jnp.float32)],
        out_shape=shapes + [jax.ShapeDtypeStruct((mp, groups, TAIL, quarter), jnp.bfloat16)],
        compiler_params=LIMIT,
        name="far_heads",
    )(*shards, *near, w_perm)
    return (outs[0] if whole else outs[:-1]), outs[-1]


def delta(mp, e, m):
    return e * mp + ((m >> 1) ^ ((m & 1) * (mp - 1)))


def plan_kernel(mp, per_pair, slots, ahead, *refs):
    len_ref, owner_ref, land_ref, start_ref, w_ref, wo_ref, tokens_ref = refs[:7]
    home_ref, table_ref, held_ref, wp_ref = refs[7:11]
    me, mine = lax.axis_index("dp"), lax.axis_index("mp")
    owners = home_ref.shape[0]
    users = len_ref.shape[1]
    chunk = -(-users // per_pair)
    top = tokens_ref.shape[0] // BLOCK - 1

    def clear(o, c):
        for i in range(4 * per_pair):
            home_ref[o, i] = 0
        return c

    lax.fori_loop(0, owners, clear, 0)
    for k in range(per_pair):

        def fill(u, c):
            o = owner_ref[0, u]
            home_ref[o, 4 * k] = len_ref[0, u]
            home_ref[o, 4 * k + 1] = start_ref[0, u]
            home_ref[o, 4 * k + 2] = land_ref[0, u]
            home_ref[o, 4 * k + 3] = u
            return c

        lax.fori_loop(k * chunk, min((k + 1) * chunk, users), fill, 0)
    copies = []
    if ahead:
        ahead_ref, sems = refs[11:]
        for i, (e, k) in enumerate(ahead):
            o = me ^ delta(mp, e, mine)
            first = i * (WINDOW + TAIL)
            ahead_ref[first + WINDOW : first + WINDOW + TAIL, :] = tail_rows(
                home_ref[o, 4 * k], home_ref[o, 4 * k + 2], tokens_ref.shape[1]
            )
            for b in range(MAXB):
                block = jnp.minimum(home_ref[o, 4 * k + 1] + b, top)
                copies.append(
                    pltpu.make_async_copy(
                        tokens_ref.at[pl.ds(pl.multiple_of(block * BLOCK, BLOCK), BLOCK), :],
                        ahead_ref.at[pl.ds(first + b * BLOCK, BLOCK), :],
                        sems.at[i * MAXB + b],
                    )
                )
                copies[-1].start()
    for i, (e, k) in enumerate(slots):
        o = me ^ delta(mp, e, mine)
        for j in range(3):
            table_ref[j * len(slots) + i] = home_ref[o, 4 * k + j]
    held_ref[...] = w_ref[...]
    part = wo_ref.shape[0] // mp
    for s in range(mp):
        start = pl.multiple_of((mine ^ s) * part, part)
        wp_ref[s * part : (s + 1) * part, :] = wo_ref[pl.ds(start, part), :]
    for copy in copies:
        copy.wait()


def plan(dp, mp, per_pair, slots, ahead, tables, w_uvqk, w_out, tokens):
    scalar = pl.BlockSpec(memory_space=pltpu.SMEM)
    local = pl.BlockSpec(memory_space=pltpu.VMEM)
    windows = [jax.ShapeDtypeStruct((len(ahead) * (WINDOW + TAIL), tokens.shape[1]), tokens.dtype)]
    windows = windows if ahead else []
    outs = pl.pallas_call(
        functools.partial(plan_kernel, mp, per_pair, slots, ahead),
        in_specs=[scalar] * len(tables) + [local] * 2 + [pl.BlockSpec(memory_space=pl.ANY)],
        out_specs=[scalar] * 2 + [local] * (2 + len(windows)),
        out_shape=[
            jax.ShapeDtypeStruct((dp, 4 * per_pair), jnp.int32),
            jax.ShapeDtypeStruct((3 * len(slots),), jnp.int32),
            jax.ShapeDtypeStruct(w_uvqk.shape, w_uvqk.dtype),
            jax.ShapeDtypeStruct(w_out.shape, w_out.dtype),
        ]
        + windows,
        scratch_shapes=[pltpu.SemaphoreType.DMA((len(ahead) * MAXB,))] * len(windows),
        compiler_params=LIMIT,
        name="plan_users",
    )(*tables, w_uvqk, w_out, tokens)
    return outs[:4], (outs[4] if ahead else None)


def place_kernel(mp, windows, states, count, home_ref, *refs):
    me, mine = lax.axis_index("dp"), lax.axis_index("mp")
    in_refs = refs[:count]
    out_ref, user_ref, users_ref, gather_ref, facts_ref, sem = refs[count:]
    for i, (array, first) in enumerate(windows):
        row = first + WINDOW
        gather_ref[i : i + 1, :] = (
            in_refs[array][row : row + TAIL, :][0:1].astype(jnp.float32).astype(jnp.int32)
        )
    out_ref[...] = jnp.zeros_like(out_ref)
    copy = pltpu.make_async_copy(gather_ref, facts_ref, sem)
    copy.start()
    users_ref[...] = jnp.zeros_like(users_ref)
    for array, first, j, e, k in states:
        o = me ^ delta(mp, e, mine ^ j)

        @pl.when(home_ref[o, 4 * k] > 0)
        def _():
            users_ref[pl.ds(home_ref[o, 4 * k + 3], 1), :] = in_refs[array][
                first : first + TAIL, :
            ].astype(jnp.float32)[0:1]

    user_ref[...] = users_ref[...].astype(user_ref.dtype)
    copy.wait()
    for i, (array, first) in enumerate(windows):
        for b in range(MAXB):

            @pl.when(facts_ref[i, 0] > b * BLOCK)
            def _():
                row = pl.multiple_of((facts_ref[i, 1] + b) * BLOCK, BLOCK)
                out_ref[pl.ds(row, BLOCK), :] = in_refs[array][
                    first + b * BLOCK : first + (b + 1) * BLOCK, :
                ]


def place(mp, windows, states, home, arrays, rows, users):
    quarter = arrays[0].shape[1]
    local = pl.BlockSpec(memory_space=pltpu.VMEM)
    return pl.pallas_call(
        functools.partial(place_kernel, mp, windows, states, len(arrays)),
        in_specs=[pl.BlockSpec(memory_space=pltpu.SMEM)] + [local] * len(arrays),
        out_specs=[local, local],
        out_shape=[
            jax.ShapeDtypeStruct((rows, quarter), jnp.bfloat16),
            jax.ShapeDtypeStruct((users, quarter), jnp.bfloat16),
        ],
        scratch_shapes=[
            pltpu.VMEM((users, quarter), jnp.float32),
            pltpu.VMEM((len(windows), quarter), jnp.int32),
            pltpu.SMEM((len(windows), quarter), jnp.int32),
            pltpu.SemaphoreType.DMA(()),
        ],
        compiler_params=LIMIT,
        name="place_blocks",
    )(home, *[in_vmem(a) for a in arrays])


def per_device(dp, mp, tokens, w_uvqk, w_out, hist_len, owner, recv_offset, block_start):
    users = hist_len.shape[1]
    per_pair = -(-users // dp)
    rounds = dp // mp
    step = WINDOW + TAIL
    upper, lower = range(rounds // 2, rounds), range(rounds // 2)
    ahead = [(e, k) for e in upper for k in range(per_pair - 1)]
    late = [(e, per_pair - 1) for e in upper]
    local = [(e, k) for e in lower for k in range(per_pair)]
    slots = late + local

    def swap(value, j):
        return lax.ppermute(value, "mp", [(i, i ^ j) for i in range(mp)])

    def send(value, e, j):
        pairs = [
            (d * mp + m, (d ^ delta(mp, e, m)) * mp + (m ^ j)) for d in range(dp) for m in range(mp)
        ]
        return lax.ppermute(value, ("dp", "mp"), pairs)

    arrays, windows, states = [], [], []

    def arrive(array, count):
        windows.extend((len(arrays), i * step) for i in range(count))
        arrays.append(array)

    tokens = in_hbm(tokens)
    held = {0: w_uvqk}
    hop = mp // 2
    while hop >= 1:
        held.update({s + hop: swap(value, hop) for s, value in list(held.items())})
        hop //= 2
    (home, table, held[0], w_perm), windows_ahead = plan(
        dp,
        mp,
        per_pair,
        slots,
        ahead,
        [in_hbm(t) for t in (hist_len, owner, recv_offset, block_start)],
        in_hbm(w_uvqk),
        in_hbm(w_out),
        tokens,
    )
    w_perm = in_vmem(w_perm)
    shards = [in_vmem(held[s]) for s in range(mp)]
    half = max(mp // 2, 1)
    sent = []
    turns = per_pair - 1
    for i in range(len(upper) if ahead else 0):
        part = windows_ahead[i * turns * step : (i + 1) * turns * step]
        sent.append(send(part, upper[i], 0))
    near = run_near_home(mp, table, tokens, shards[:half], len(slots))
    out, late_state = run_far(mp, shards[half:], near, w_perm, 0, len(late), True)
    held_late = []
    for i, (e, _) in enumerate(late):
        held_late.append(send(out[:, i * step : (i + 1) * step], e, 0))
    outs, local_state = run_far(mp, shards[half:], near, w_perm, len(late), len(local), False)
    for e in lower:
        for j in range(mp):
            first = e * per_pair * step
            arrive(send(outs[j][first : first + per_pair * step], e, j), per_pair)
    parts = [late_state, local_state]
    order = slots
    for i, e in enumerate(upper if ahead else ()):
        near = run_near_owner(mp, sent[i], shards[:half], turns)
        outs, state = run_far(mp, shards[half:], near, w_perm, 0, turns, False)
        parts.append(send(state, e, 0))
        order = order + [(e, k) for k in range(turns)]
        for j in range(mp):
            arrive(swap(outs[j], j) if j else outs[j], turns)
    for j in range(mp):
        pieces = [value[j] for value in held_late]
        pieces += [part[j].reshape(-1, part.shape[-1]) for part in parts]
        joined = jnp.concatenate(pieces, 0)
        joined = swap(joined, j) if j else joined
        base = len(late) * step
        states += [
            (len(arrays), base + i * TAIL, j, e, k) for i, (e, k) in enumerate(order)
        ]
        arrive(joined, len(late))
    return place(mp, windows, states, home, arrays, tokens.shape[0], users)


def solution(mesh):
    dp, mp = mesh.shape["dp"], mesh.shape["mp"]
    in_specs = (
        P("dp", None),
        P(None, "mp"),
        P(),
        P("dp", None),
        P("dp", None),
        P("dp", None),
        P("dp", None),
    )
    out_specs = (P("dp", "mp"), P("dp", "mp"))
    return jax.shard_map(
        functools.partial(per_device, dp, mp),
        mesh=mesh,
        in_specs=in_specs,
        out_specs=out_specs,
        check_vma=False,
    )
```

profile of v0, /device:TPU:0, one launch (start us, length us, event | category | flops | bytes accessed | tf_op | source)
XLA Modules:
  0.0 82.0 jit_solution(6982152623025965047)
XLA Ops:
  0.6 3.0 %collective-permute-start = (bf16[512,512]{1,0:T(8,128)(2,1)}, bf16[512,512]{1,0:T(8,128)(2,1)S(1)}, u32[]{:S(2)}, u32[]{:S(2)}) collective-permute-start(bf16[512,512]{1,0:T(8,128)(2,1)} %refs_4_.1), channel_id=1, source_target_pairs={{0,2},{1,3},{2,0},{3,1},{4,6},{5,7},{6,4},{7,5},{8,10},{9,11},{10,... | collective-permute-start | bytes 1572872 | tf_op jit(solution)/shard_map/ppermute | solution.py:386
  3.7 3.4 %plan_users.1 = (s32[8,12]{1,0:T(8,128)S(1)}, s32[12]{0:T(128)S(1)}, bf16[512,512]{1,0:T(8,128)(2,1)S(1)}, bf16[512,512]{1,0:T(8,128)(2,1)S(1)}, bf16[528,512]{1,0:T(8,128)(2,1)S(1)}) custom-call(s32[1,24]{1,0:T(1,128)} %refs_0_.2, s32[1,24]{1,0:T(1,128)} %refs_1_.2, s32[1,24]{1,0:T(1,128)} %refs_2_.1, s32[1,24]{1,0:T(1,128)} %refs_3_.1, ...), custom_call_target="tpu_custom_call" | custom-call | tf_op jit(solution)/shard_map/plan_users/pallas_call | solution.py:299
  7.1 2.7 %collective-permute-start.7 = (bf16[528,512]{1,0:T(8,128)(2,1)S(1)}, bf16[528,512]{1,0:T(8,128)(2,1)S(1)}, u32[]{:S(2)}, u32[]{:S(2)}) collective-permute-start(bf16[528,512]{1,0:T(8,128)(2,1)S(1)} %get-tuple-element.42), channel_id=1, source_target_pairs={{0,16},{1,29},{2,22},{3,27},{4,20},{5,25},{6,18},{7,31},{8,24},{9,... | collective-permute-start | bytes 1622024 | tf_op jit(solution)/shard_map/ppermute | solution.py:392
  9.7 1.2 %collective-permute-start.2 = (bf16[512,512]{1,0:T(8,128)(2,1)S(1)}, bf16[512,512]{1,0:T(8,128)(2,1)S(1)}, u32[]{:S(2)}, u32[]{:S(2)}) collective-permute-start(bf16[512,512]{1,0:T(8,128)(2,1)S(1)} %copy-done), channel_id=1, source_target_pairs={{0,1},{1,0},{2,3},{3,2},{4,5},{5,4},{6,7},{7,6},{8,9},{9,8},{10,11... | collective-permute-start | bytes 1572872 | tf_op jit(solution)/shard_map/ppermute | solution.py:386
  11.0 4.8 %collective-permute-done.refs_0_ = bf16[512,512]{1,0:T(8,128)(2,1)S(1)} collective-permute-done((bf16[512,512]{1,0:T(8,128)(2,1)}, bf16[512,512]{1,0:T(8,128)(2,1)S(1)}, u32[]{:S(2)}, u32[]{:S(2)}) %collective-permute-start) | collective-permute-done | bytes 524320 | tf_op jit(solution)/shard_map/ppermute | solution.py:386
  15.8 0.0 collective-permute-start.1
  15.8 0.0 collective-permute-done.2.refs_3_.refs_2_
  15.8 6.5 %near_home.1 = (bf16[1024,512]{1,0:T(8,128)(2,1)S(1)}, bf16[1024,512]{1,0:T(8,128)(2,1)S(1)}, f32[1024,256]{1,0:T(8,128)S(1)}, bf16[1024,256]{1,0:T(8,128)(2,1)S(1)}, bf16[32,128]{1,0:T(8,128)(2,1)S(1)}) custom-call(s32[12]{0:T(128)S(1)} %get-tuple-element.30.table_ref, bf16[6144,512]{1,0:T(8,128)(2,1)} %refs_1_.3, bf16[6144,512]{1,0:T(8,128)(2,1)} %refs_1_.3, ...), custom_call_target="tpu_custom_call" | custom-call | tf_op jit(solution)/shard_map/near_home/pallas_call | solution.py:175
  22.3 12.3 %collective-permute-done.7.refs_0_ = bf16[528,512]{1,0:T(8,128)(2,1)S(1)} collective-permute-done((bf16[528,512]{1,0:T(8,128)(2,1)S(1)}, bf16[528,512]{1,0:T(8,128)(2,1)S(1)}, u32[]{:S(2)}, u32[]{:S(2)}) %collective-permute-start.7) | collective-permute-done | bytes 540704 | tf_op jit(solution)/shard_map/ppermute | solution.py:392
  34.6 2.4 %near_owner.1 = (bf16[512,512]{1,0:T(8,128)(2,1)S(1)}, bf16[512,512]{1,0:T(8,128)(2,1)S(1)}, f32[512,256]{1,0:T(8,128)S(1)}, bf16[512,256]{1,0:T(8,128)(2,1)S(1)}, bf16[16,128]{1,0:T(8,128)(2,1)S(1)}) custom-call(bf16[528,512]{1,0:T(8,128)(2,1)S(1)} %collective-permute-done.7.refs_0_, bf16[512,512]{1,0:T(8,128)(2,1)S(1)} %get-tuple-element.31.refs_2_.refs_1_, ...), custom_call_target="tpu_custom_call" | custom-call | tf_op jit(solution)/shard_map/near_owner/pallas_call | solution.py:197
  37.1 3.1 %far_heads.4 = (bf16[528,128]{1,0:T(8,128)(2,1)S(1)}, bf16[528,128]{1,0:T(8,128)(2,1)S(1)}, bf16[528,128]{1,0:T(8,128)(2,1)S(1)}, bf16[528,128]{1,0:T(8,128)(2,1)S(1)}, bf16[4,2,8,128]{3,2,1,0:T(8,128)(2,1)S(1)}) custom-call(bf16[512,512]{1,0:T(8,128)(2,1)S(1)} %collective-permute-done.refs_0_, bf16[512,512]{1,0:T(8,128)(2,1)S(1)} %collective-permute-done.1.refs_1_, ...), custom_call_target="tpu_custom_call" | custom-call | tf_op jit(solution)/shard_map/far_heads/pallas_call | solution.py:219
  40.1 0.1 collective-permute-start.12
  40.2 0.1 collective-permute-start.8
  40.3 0.4 collective-permute-start.9
  40.7 1.4 %collective-permute-start.10 = (bf16[528,128]{1,0:T(8,128)(2,1)S(1)}, bf16[528,128]{1,0:T(8,128)(2,1)S(1)}, u32[]{:S(2)}, u32[]{:S(2)}) collective-permute-start(bf16[528,128]{1,0:T(8,128)(2,1)S(1)} %get-tuple-element.51), channel_id=1, source_target_pairs={{0,3},{1,2},{2,1},{3,0},{4,7},{5,6},{6,5},{7,4},{8,11},{9,10},{10,... | collective-permute-start | bytes 405512 | tf_op jit(solution)/shard_map/ppermute | solution.py:386
  42.1 4.5 %far_heads.3 = (bf16[792,128]{1,0:T(8,128)(2,1)S(1)}, bf16[792,128]{1,0:T(8,128)(2,1)S(1)}, bf16[792,128]{1,0:T(8,128)(2,1)S(1)}, bf16[792,128]{1,0:T(8,128)(2,1)S(1)}, bf16[4,3,8,128]{3,2,1,0:T(8,128)(2,1)S(1)}) custom-call(bf16[512,512]{1,0:T(8,128)(2,1)S(1)} %collective-permute-done.refs_0_, bf16[512,512]{1,0:T(8,128)(2,1)S(1)} %collective-permute-done.1.refs_1_, ...), custom_call_target="tpu_custom_call" | custom-call | tf_op jit(solution)/shard_map/far_heads/pallas_call | solution.py:219
  46.7 1.5 %far_heads.5 = (bf16[4,264,128]{2,1,0:T(8,128)(2,1)S(1)}, bf16[4,1,8,128]{3,2,1,0:T(8,128)(2,1)S(1)}) custom-call(bf16[512,512]{1,0:T(8,128)(2,1)S(1)} %collective-permute-done.refs_0_, bf16[512,512]{1,0:T(8,128)(2,1)S(1)} %collective-permute-done.1.refs_1_, bf16[1024,512]{1,0:T(8,128)(2,1)S(1)} %get-tuple-element.32.refs_2_, ...), custom_call_target="tpu_custom_call" | custom-call | tf_op jit(solution)/shard_map/far_heads/pallas_call | solution.py:219
  48.2 2.9 %collective-permute-start.11 = (bf16[4,264,128]{2,1,0:T(8,128)(2,1)S(1)}, bf16[4,264,128]{2,1,0:T(8,128)(2,1)S(1)}, u32[]{:S(2)}, u32[]{:S(2)}) collective-permute-start(bf16[4,264,128]{2,1,0:T(8,128)(2,1)S(1)} %get-tuple-element.52), channel_id=1, source_target_pairs={{0,16},{1,29},{2,22},{3,27},{4,20},{5,25},{6,18},{7,31},{8,24},{9,... | collective-permute-start | bytes 811016 | tf_op jit(solution)/shard_map/ppermute | solution.py:392
  51.1 0.0 collective-permute-done.12
  51.1 0.7 collective-permute-start.3
  51.8 12.2 %collective-permute-done.11 = bf16[4,264,128]{2,1,0:T(8,128)(2,1)S(1)} collective-permute-done((bf16[4,264,128]{2,1,0:T(8,128)(2,1)S(1)}, bf16[4,264,128]{2,1,0:T(8,128)(2,1)S(1)}, u32[]{:S(2)}, u32[]{:S(2)}) %collective-permute-start.11) | collective-permute-done | bytes 270368 | tf_op jit(solution)/shard_map/ppermute | solution.py:392
  64.0 0.0 collective-permute-done.8.refs_5_
  64.0 0.9 %collective-permute-start.5 = (bf16[792,128]{1,0:T(8,128)(2,1)S(1)}, bf16[792,128]{1,0:T(8,128)(2,1)S(1)}, u32[]{:S(2)}, u32[]{:S(2)}) collective-permute-start(bf16[792,128]{1,0:T(8,128)(2,1)S(1)} %get-tuple-element.40), channel_id=1, source_target_pairs={{0,2},{1,15},{2,4},{3,9},{4,6},{5,11},{6,0},{7,13},{8,10},{9,7},{1... | collective-permute-start | bytes 608264 | tf_op jit(solution)/shard_map/ppermute | solution.py:392
  65.0 1.0 %collective-permute-start.6 = (bf16[792,128]{1,0:T(8,128)(2,1)S(1)}, bf16[792,128]{1,0:T(8,128)(2,1)S(1)}, u32[]{:S(2)}, u32[]{:S(2)}) collective-permute-start(bf16[792,128]{1,0:T(8,128)(2,1)S(1)} %get-tuple-element.41), channel_id=1, source_target_pairs={{0,3},{1,14},{2,5},{3,8},{4,7},{5,10},{6,1},{7,12},{8,11},{9,6},{1... | collective-permute-start | bytes 608264 | tf_op jit(solution)/shard_map/ppermute | solution.py:392
  65.9 1.6 %collective-permute-start.13 = (bf16[312,128]{1,0:T(8,128)(2,1)S(1)}, bf16[312,128]{1,0:T(8,128)(2,1)S(1)}, u32[]{:S(2)}, u32[]{:S(2)}) collective-permute-start(bf16[312,128]{1,0:T(8,128)(2,1)S(1)} %pad_maximum_fusion.1), channel_id=1, source_target_pairs={{0,1},{1,0},{2,3},{3,2},{4,5},{5,4},{6,7},{7,6},{8,9},{9,8},{10,11... | collective-permute-start | bytes 239624 | tf_op jit(solution)/shard_map/ppermute | solution.py:386
  67.6 1.4 %collective-permute-start.14 = (bf16[312,128]{1,0:T(8,128)(2,1)S(1)}, bf16[312,128]{1,0:T(8,128)(2,1)S(1)}, u32[]{:S(2)}, u32[]{:S(2)}) collective-permute-start(bf16[312,128]{1,0:T(8,128)(2,1)S(1)} %pad_maximum_fusion.2), channel_id=1, source_target_pairs={{0,2},{1,3},{2,0},{3,1},{4,6},{5,7},{6,4},{7,5},{8,10},{9,11},{10,... | collective-permute-start | bytes 239624 | tf_op jit(solution)/shard_map/ppermute | solution.py:386
  69.0 2.2 %collective-permute-done.4.refs_1_ = bf16[792,128]{1,0:T(8,128)(2,1)S(1)} collective-permute-done((bf16[792,128]{1,0:T(8,128)(2,1)S(1)}, bf16[792,128]{1,0:T(8,128)(2,1)S(1)}, u32[]{:S(2)}, u32[]{:S(2)}) %collective-permute-start.4) | collective-permute-done | bytes 202784 | tf_op jit(solution)/shard_map/ppermute | solution.py:392
  71.2 0.0 collective-permute-start.15
  71.2 4.9 %collective-permute-done.5.refs_2_ = bf16[792,128]{1,0:T(8,128)(2,1)S(1)} collective-permute-done((bf16[792,128]{1,0:T(8,128)(2,1)S(1)}, bf16[792,128]{1,0:T(8,128)(2,1)S(1)}, u32[]{:S(2)}, u32[]{:S(2)}) %collective-permute-start.5) | collective-permute-done | bytes 202784 | tf_op jit(solution)/shard_map/ppermute | solution.py:392
  76.1 0.3 collective-permute-done.6.refs_3_
  76.5 2.3 %collective-permute-done.14.refs_10_ = bf16[312,128]{1,0:T(8,128)(2,1)S(1)} collective-permute-done((bf16[312,128]{1,0:T(8,128)(2,1)S(1)}, bf16[312,128]{1,0:T(8,128)(2,1)S(1)}, u32[]{:S(2)}, u32[]{:S(2)}) %collective-permute-start.14) | collective-permute-done | bytes 79904 | tf_op jit(solution)/shard_map/ppermute | solution.py:386
  78.8 3.2 %place_blocks.1 = (bf16[6144,128]{1,0:T(8,128)(2,1)}, bf16[24,128]{1,0:T(8,128)(2,1)}) custom-call(s32[8,12]{1,0:T(8,128)S(1)} %get-tuple-element.29.home_ref, bf16[792,128]{1,0:T(8,128)(2,1)S(1)} %collective-permute-done.3.refs_0_, bf16[792,128]{1,0:T(8,128)(2,1)S(1)} %collective-permute-done.4.refs_1_, ...), custom_call_target="tpu_custom_call" | custom-call | tf_op jit(solution)/shard_map/place_blocks/pallas_call | solution.py:355
  (17 shorter events, 0.1 us)
Async XLA Ops:
  0.6 9.1 %copy-start = (bf16[512,512]{1,0:T(8,128)(2,1)S(1)}, bf16[512,512]{1,0:T(8,128)(2,1)}, u32[]{:S(2)}) copy-start(bf16[512,512]{1,0:T(8,128)(2,1)} %refs_4_.1) | copy-start | bytes 1572868
  0.6 15.2 %collective-permute-start = (bf16[512,512]{1,0:T(8,128)(2,1)}, bf16[512,512]{1,0:T(8,128)(2,1)S(1)}, u32[]{:S(2)}, u32[]{:S(2)}) collective-permute-start(bf16[512,512]{1,0:T(8,128)(2,1)} %refs_4_.1), channel_id=1, source_target_pairs={{0,2},{1,3},{2,0},{3,1},{4,6},{5,7},{6,4},{7,5},{8,10},{9,11},{10,... | collective-permute-start | bytes 1572872 | tf_op jit(solution)/shard_map/ppermute | solution.py:386
  7.1 27.5 %collective-permute-start.7 = (bf16[528,512]{1,0:T(8,128)(2,1)S(1)}, bf16[528,512]{1,0:T(8,128)(2,1)S(1)}, u32[]{:S(2)}, u32[]{:S(2)}) collective-permute-start(bf16[528,512]{1,0:T(8,128)(2,1)S(1)} %get-tuple-element.42), channel_id=1, source_target_pairs={{0,16},{1,29},{2,22},{3,27},{4,20},{5,25},{6,18},{7,31},{8,24},{9,... | collective-permute-start | bytes 1622024 | tf_op jit(solution)/shard_map/ppermute | solution.py:392
  9.7 6.1 %collective-permute-start.2 = (bf16[512,512]{1,0:T(8,128)(2,1)S(1)}, bf16[512,512]{1,0:T(8,128)(2,1)S(1)}, u32[]{:S(2)}, u32[]{:S(2)}) collective-permute-start(bf16[512,512]{1,0:T(8,128)(2,1)S(1)} %copy-done), channel_id=1, source_target_pairs={{0,1},{1,0},{2,3},{3,2},{4,5},{5,4},{6,7},{7,6},{8,9},{9,8},{10,11... | collective-permute-start | bytes 1572872 | tf_op jit(solution)/shard_map/ppermute | solution.py:386
  15.8 21.2 %collective-permute-start.1 = (bf16[512,512]{1,0:T(8,128)(2,1)S(1)}, bf16[512,512]{1,0:T(8,128)(2,1)S(1)}, u32[]{:S(2)}, u32[]{:S(2)}) collective-permute-start(bf16[512,512]{1,0:T(8,128)(2,1)S(1)} %collective-permute-done.refs_0_), channel_id=1, source_target_pairs={{0,1},{1,0},{2,3},{3,2},{4,5},{5,4},{6,7},{7,6},{8,9},{9,8},{10,11... | collective-permute-start | bytes 1572872 | tf_op jit(solution)/shard_map/ppermute | solution.py:386
  40.1 11.0 %collective-permute-start.12 = (bf16[4,2,8,128]{3,2,1,0:T(8,128)(2,1)S(1)}, bf16[4,2,8,128]{3,2,1,0:T(8,128)(2,1)S(1)}, u32[]{:S(2)}, u32[]{:S(2)}) collective-permute-start(bf16[4,2,8,128]{3,2,1,0:T(8,128)(2,1)S(1)} %get-tuple-element.55), channel_id=1, source_target_pairs={{0,16},{1,29},{2,22},{3,27},{4,20},{5,25},{6,18},{7,31},{8,24},{9,... | collective-permute-start | bytes 49160 | tf_op jit(solution)/shard_map/ppermute | solution.py:392
  40.2 23.8 %collective-permute-start.8 = (bf16[528,128]{1,0:T(8,128)(2,1)S(1)}, bf16[528,128]{1,0:T(8,128)(2,1)S(1)}, u32[]{:S(2)}, u32[]{:S(2)}) collective-permute-start(bf16[528,128]{1,0:T(8,128)(2,1)S(1)} %get-tuple-element.49), channel_id=1, source_target_pairs={{0,1},{1,0},{2,3},{3,2},{4,5},{5,4},{6,7},{7,6},{8,9},{9,8},{10,11... | collective-permute-start | bytes 405512 | tf_op jit(solution)/shard_map/ppermute | solution.py:386
  40.3 24.7 %collective-permute-start.9 = (bf16[528,128]{1,0:T(8,128)(2,1)S(1)}, bf16[528,128]{1,0:T(8,128)(2,1)S(1)}, u32[]{:S(2)}, u32[]{:S(2)}) collective-permute-start(bf16[528,128]{1,0:T(8,128)(2,1)S(1)} %get-tuple-element.50), channel_id=1, source_target_pairs={{0,2},{1,3},{2,0},{3,1},{4,6},{5,7},{6,4},{7,5},{8,10},{9,11},{10,... | collective-permute-start | bytes 405512 | tf_op jit(solution)/shard_map/ppermute | solution.py:386
  40.7 25.2 %collective-permute-start.10 = (bf16[528,128]{1,0:T(8,128)(2,1)S(1)}, bf16[528,128]{1,0:T(8,128)(2,1)S(1)}, u32[]{:S(2)}, u32[]{:S(2)}) collective-permute-start(bf16[528,128]{1,0:T(8,128)(2,1)S(1)} %get-tuple-element.51), channel_id=1, source_target_pairs={{0,3},{1,2},{2,1},{3,0},{4,7},{5,6},{6,5},{7,4},{8,11},{9,10},{10,... | collective-permute-start | bytes 405512 | tf_op jit(solution)/shard_map/ppermute | solution.py:386
  48.2 15.8 %collective-permute-start.11 = (bf16[4,264,128]{2,1,0:T(8,128)(2,1)S(1)}, bf16[4,264,128]{2,1,0:T(8,128)(2,1)S(1)}, u32[]{:S(2)}, u32[]{:S(2)}) collective-permute-start(bf16[4,264,128]{2,1,0:T(8,128)(2,1)S(1)} %get-tuple-element.52), channel_id=1, source_target_pairs={{0,16},{1,29},{2,22},{3,27},{4,20},{5,25},{6,18},{7,31},{8,24},{9,... | collective-permute-start | bytes 811016 | tf_op jit(solution)/shard_map/ppermute | solution.py:392
  51.1 16.5 %collective-permute-start.3 = (bf16[792,128]{1,0:T(8,128)(2,1)S(1)}, bf16[792,128]{1,0:T(8,128)(2,1)S(1)}, u32[]{:S(2)}, u32[]{:S(2)}) collective-permute-start(bf16[792,128]{1,0:T(8,128)(2,1)S(1)} %get-tuple-element.38), channel_id=1, source_target_pairs={{0,0},{1,13},{2,6},{3,11},{4,4},{5,9},{6,2},{7,15},{8,8},{9,5},{10... | collective-permute-start | bytes 608264 | tf_op jit(solution)/shard_map/ppermute | solution.py:392
  64.0 7.2 %collective-permute-start.4 = (bf16[792,128]{1,0:T(8,128)(2,1)S(1)}, bf16[792,128]{1,0:T(8,128)(2,1)S(1)}, u32[]{:S(2)}, u32[]{:S(2)}) collective-permute-start(bf16[792,128]{1,0:T(8,128)(2,1)S(1)} %get-tuple-element.39), channel_id=1, source_target_pairs={{0,1},{1,12},{2,7},{3,10},{4,5},{5,8},{6,3},{7,14},{8,9},{9,4},{10... | collective-permute-start | bytes 608264 | tf_op jit(solution)/shard_map/ppermute | solution.py:392
  64.0 12.1 %collective-permute-start.5 = (bf16[792,128]{1,0:T(8,128)(2,1)S(1)}, bf16[792,128]{1,0:T(8,128)(2,1)S(1)}, u32[]{:S(2)}, u32[]{:S(2)}) collective-permute-start(bf16[792,128]{1,0:T(8,128)(2,1)S(1)} %get-tuple-element.40), channel_id=1, source_target_pairs={{0,2},{1,15},{2,4},{3,9},{4,6},{5,11},{6,0},{7,13},{8,10},{9,7},{1... | collective-permute-start | bytes 608264 | tf_op jit(solution)/shard_map/ppermute | solution.py:392
  65.0 11.5 %collective-permute-start.6 = (bf16[792,128]{1,0:T(8,128)(2,1)S(1)}, bf16[792,128]{1,0:T(8,128)(2,1)S(1)}, u32[]{:S(2)}, u32[]{:S(2)}) collective-permute-start(bf16[792,128]{1,0:T(8,128)(2,1)S(1)} %get-tuple-element.41), channel_id=1, source_target_pairs={{0,3},{1,14},{2,5},{3,8},{4,7},{5,10},{6,1},{7,12},{8,11},{9,6},{1... | collective-permute-start | bytes 608264 | tf_op jit(solution)/shard_map/ppermute | solution.py:392
  65.9 10.5 %collective-permute-start.13 = (bf16[312,128]{1,0:T(8,128)(2,1)S(1)}, bf16[312,128]{1,0:T(8,128)(2,1)S(1)}, u32[]{:S(2)}, u32[]{:S(2)}) collective-permute-start(bf16[312,128]{1,0:T(8,128)(2,1)S(1)} %pad_maximum_fusion.1), channel_id=1, source_target_pairs={{0,1},{1,0},{2,3},{3,2},{4,5},{5,4},{6,7},{7,6},{8,9},{9,8},{10,11... | collective-permute-start | bytes 239624 | tf_op jit(solution)/shard_map/ppermute | solution.py:386
  67.6 11.2 %collective-permute-start.14 = (bf16[312,128]{1,0:T(8,128)(2,1)S(1)}, bf16[312,128]{1,0:T(8,128)(2,1)S(1)}, u32[]{:S(2)}, u32[]{:S(2)}) collective-permute-start(bf16[312,128]{1,0:T(8,128)(2,1)S(1)} %pad_maximum_fusion.2), channel_id=1, source_target_pairs={{0,2},{1,3},{2,0},{3,1},{4,6},{5,7},{6,4},{7,5},{8,10},{9,11},{10,... | collective-permute-start | bytes 239624 | tf_op jit(solution)/shard_map/ppermute | solution.py:386
  71.2 7.6 %collective-permute-start.15 = (bf16[312,128]{1,0:T(8,128)(2,1)S(1)}, bf16[312,128]{1,0:T(8,128)(2,1)S(1)}, u32[]{:S(2)}, u32[]{:S(2)}) collective-permute-start(bf16[312,128]{1,0:T(8,128)(2,1)S(1)} %pad_maximum_fusion.3), channel_id=1, source_target_pairs={{0,3},{1,2},{2,1},{3,0},{4,7},{5,6},{6,5},{7,4},{8,11},{9,10},{10,... | collective-permute-start | bytes 239624 | tf_op jit(solution)/shard_map/ppermute | solution.py:386
where the time goes:
time: 82.4 us; the launch traced here: 82 us
  waiting for transfers between devices  39.1 us (47%)
  Pallas kernels  24.6 us (30%)
  starting transfers between devices  17.4 us (21%)
    ppermute x7, waiting for transfers between devices, send(): return lax.ppermute(value, ('dp', 'mp'), pairs)  32 us
    ppermute x9, starting transfers between devices, swap(): return lax.ppermute(value, 'mp', [(i, i ^ j) for i in range(mp)])  9.22 us
    pallas_call x3, Pallas kernels, run_far(): pl.pallas_call(functools.partial(far_kernel, mp, len(shards), base, whole...  9.09 us
    ppermute x7, starting transfers between devices, send(): return lax.ppermute(value, ('dp', 'mp'), pairs)  8.19 us
    ppermute x9, waiting for transfers between devices, swap(): return lax.ppermute(value, 'mp', [(i, i ^ j) for i in range(mp)])  7.13 us
    pallas_call x1, Pallas kernels, run_near_home(): pl.pallas_call(functools.partial(near_home_kernel, len(shards), slots), g...  6.48 us
    pallas_call x1, Pallas kernels, plan(): pl.pallas_call(functools.partial(plan_kernel, mp, per_pair, slots, ahead)...  3.41 us
    pallas_call x1, Pallas kernels, place(): pl.pallas_call(functools.partial(place_kernel, mp, windows, states, len(a...  3.24 us
  transfers between devices with their start and end apart: 16, of which 7 were waited for; matrix products, arithmetic and copies ran while one was open for 0% of the time, Pallas kernels for 22%

commit v1 on v0

v1 whole, which is shorter than its diff:
```python
import functools

import jax
import jax.numpy as jnp
from jax import lax
from jax.experimental import pallas as pl
from jax.experimental.pallas import tpu as pltpu
from jax.sharding import PartitionSpec as P


BLOCK = 128
MAXB = 2
HEAD = 128
WINDOW = MAXB * BLOCK
TAIL = 8
EPS = 1e-05
LIMIT = pltpu.CompilerParams(vmem_limit_bytes=24 * 1024 * 1024)


def in_vmem(value):
    return pltpu.with_memory_space_constraint(value, pltpu.VMEM)


def in_hbm(value):
    return pltpu.with_memory_space_constraint(value, pltpu.HBM)


def half_silu(half):
    return half + half * jnp.tanh(half)


def norm_scale(total, squares, width):
    average = total * (1.0 / width)
    variance = squares * (1.0 / width) - average * average
    return average, lax.rsqrt(variance + EPS)


def norm_half(widened):
    average, scale = norm_scale(
        jnp.sum(widened, 1, keepdims=True),
        jnp.sum(widened * widened, 1, keepdims=True),
        widened.shape[1],
    )
    return ((widened - average) * (0.5 * scale)).astype(jnp.bfloat16)


def attend_heads(halved, w_refs):
    row = lax.broadcasted_iota(jnp.int32, (BLOCK, BLOCK), 0)
    col = lax.broadcasted_iota(jnp.int32, (BLOCK, BLOCK), 1)
    causal = col <= row
    half_scale = 0.5 * HEAD ** (-0.5)
    heads = [
        w_ref[:, head * 4 * HEAD : (head + 1) * 4 * HEAD]
        for w_ref in w_refs
        for head in range(w_ref.shape[1] // (4 * HEAD))
    ]
    halves = [jnp.dot(halved, w, preferred_element_type=jnp.float32) for w in heads]
    projs = [half_silu(half).astype(jnp.bfloat16) for half in halves]
    split = [[proj[:, i * HEAD : (i + 1) * HEAD] for i in range(4)] for proj in projs]
    raws = [
        lax.dot_general(q, k, (((1,), (1,)), ((), ())), preferred_element_type=jnp.float32)
        for _, _, q, k in split
    ]
    values = []
    for raw, (_, v, _, _) in zip(raws, split):
        weights = []
        for b in range(MAXB):
            rows = slice(b * BLOCK, (b + 1) * BLOCK)
            act = half_silu(raw[rows, : (b + 1) * BLOCK] * half_scale)
            pieces = [act[:, : b * BLOCK]] if b > 0 else []
            pieces.append(jnp.where(causal, act[:, b * BLOCK :], 0.0))
            if b + 1 < MAXB:
                pieces.append(jnp.zeros((BLOCK, WINDOW - (b + 1) * BLOCK), jnp.float32))
            weights.append(jnp.concatenate(pieces, 1).astype(jnp.bfloat16))
        values.append(jnp.dot(jnp.concatenate(weights, 0), v, preferred_element_type=jnp.float32))
    return values, [u for u, _, _, _ in split]


def near_rows(base, widened, w_refs, out_refs):
    rows_ref, half_ref, value_ref, gate_ref = out_refs
    rows = pl.ds(pl.multiple_of(base * WINDOW, WINDOW), WINDOW)
    halved = norm_half(widened)
    rows_ref[rows, :] = widened.astype(rows_ref.dtype)
    half_ref[rows, :] = halved
    values, gates = attend_heads(halved, w_refs)
    value_ref[rows, :] = jnp.concatenate(values, 1)
    gate_ref[rows, :] = jnp.concatenate(gates, 1)


def near_home_kernel(mp, near, base, total_slots, table_ref, *refs):
    block_refs, w_refs = refs[:MAXB], refs[MAXB : MAXB + near]
    near_refs = refs[MAXB + near :]
    slot = pl.program_id(0)
    if base == 0:
        wo_ref, *near_refs, held_ref, wp_ref = near_refs

        @pl.when(slot == 0)
        def _():
            mine = lax.axis_index("mp")
            held_ref[...] = w_refs[0][...]
            part = wo_ref.shape[0] // mp
            for s in range(mp):
                start = pl.multiple_of((mine ^ s) * part, part)
                wp_ref[s * part : (s + 1) * part, :] = wo_ref[pl.ds(start, part), :]

    tail_ref = near_refs[-1]
    tail_ref[pl.ds(pl.multiple_of(slot * TAIL, TAIL), TAIL), :] = tail_rows(
        table_ref[base + slot], table_ref[2 * total_slots + base + slot], tail_ref.shape[1]
    )
    widened = jnp.concatenate([ref[...] for ref in block_refs], 0).astype(jnp.float32)
    near_rows(slot, widened, w_refs, near_refs[:-1])


def near_owner_kernel(near, *refs):
    arrived_ref, w_refs = refs[0], refs[1 : 1 + near]
    tail_ref = refs[-1]
    slot = pl.program_id(0)
    first = pl.multiple_of(slot * (WINDOW + TAIL), TAIL)
    tail_ref[pl.ds(pl.multiple_of(slot * TAIL, TAIL), TAIL), :] = arrived_ref[
        pl.ds(first + WINDOW, TAIL), : tail_ref.shape[1]
    ]
    near_rows(slot, arrived_ref[pl.ds(first, WINDOW), :].astype(jnp.float32), w_refs, refs[1 + near : -1])


def far_kernel(mp, far, base, paired, joined, riders, *refs):
    w_refs = refs[:far]
    rows_ref, half_ref, near_value_ref, near_gate_ref, tail_ref, wp_ref = refs[far : far + 6]
    stated = paired is not False
    earlier = refs[far + 6 : far + 6 + (mp if joined else 0)]
    taken = far + 6 + len(earlier)
    rider_refs = refs[taken : taken + riders]
    out_refs = refs[taken + riders : -2]
    state_ref, mixed_ref = refs[-2:]
    if not stated:
        out_refs, state_ref = refs[taken + riders : -1], None
    if paired:
        out_refs = [out_refs[s // 2].at[s % 2] for s in range(mp)]
    for out_ref, early_ref in zip(out_refs, earlier):
        out_ref[: joined * (WINDOW + TAIL), :] = early_ref[...]
    row = (joined + pl.num_programs(0)) * (WINDOW + TAIL) if riders else 0
    for rider_ref in rider_refs:
        for i in range(rider_ref.shape[1]):
            for s in range(mp):
                out_refs[s][pl.ds(pl.multiple_of(row, TAIL), TAIL), :] = rider_ref[s, i]
            row += TAIL
    slot = pl.program_id(0)
    mine = lax.axis_index("mp")
    width = wp_ref.shape[0]
    rows = pl.ds(pl.multiple_of((base + slot) * WINDOW, WINDOW), WINDOW)
    tail = tail_ref[pl.ds(pl.multiple_of((base + slot) * TAIL, TAIL), TAIL), :]
    length = tail.astype(jnp.float32)[0:1, 0:1]
    values, gates = attend_heads(half_ref[rows, :], w_refs)
    value = jnp.concatenate([near_value_ref[rows, :]] + values, 1)
    gate = jnp.concatenate([near_gate_ref[rows, :]] + gates, 1)
    average, scale = norm_scale(
        jnp.sum(value, 1, keepdims=True) * (1.0 / WINDOW),
        jnp.sum(value * value, 1, keepdims=True) * (1.0 / WINDOW**2),
        width,
    )
    average, scale = average * WINDOW, scale * (1.0 / WINDOW)
    gated = (value - average) * scale * gate.astype(jnp.float32)
    widened = rows_ref[rows, :].astype(jnp.float32)
    live = lax.broadcasted_iota(jnp.int32, (WINDOW, 1), 0).astype(jnp.float32)
    final = live == length - 1.0
    quarter = width // mp
    if paired is None:
        last_gated = jnp.sum(jnp.where(final, gated, 0.0), 0, keepdims=True)
        last_row = jnp.sum(jnp.where(final, widened, 0.0), 0, keepdims=True)
        mixed_ref[WINDOW:, :] = jnp.broadcast_to(last_row, (TAIL, width)) + jnp.dot(
            jnp.broadcast_to(last_gated, (TAIL, width)).astype(jnp.bfloat16),
            wp_ref[...],
            preferred_element_type=jnp.float32,
        )
        for s in range(mp):
            start = pl.multiple_of((mine ^ s) * quarter, quarter)
            state_ref[s, slot] = mixed_ref[WINDOW:, pl.ds(start, quarter)].astype(jnp.bfloat16)
        return
    mixed = widened + jnp.dot(
        gated.astype(jnp.bfloat16), wp_ref[...], preferred_element_type=jnp.float32
    )
    mixed_ref[:WINDOW, :] = jnp.where(live < length, mixed, 0.0)
    last_row = jnp.sum(jnp.where(final, mixed, 0.0), 0, keepdims=True)
    mixed_ref[WINDOW:, :] = jnp.broadcast_to(last_row, (TAIL, width))
    first = pl.multiple_of((joined + slot) * (WINDOW + TAIL), TAIL)
    for s in range(mp):
        start = pl.multiple_of((mine ^ s) * quarter, quarter)
        out_refs[s][pl.ds(first, WINDOW), :] = mixed_ref[:WINDOW, pl.ds(start, quarter)].astype(
            jnp.bfloat16
        )
        out_refs[s][pl.ds(first + WINDOW, TAIL), :] = tail
        if stated:
            state_ref[s, slot] = mixed_ref[WINDOW:, pl.ds(start, quarter)].astype(jnp.bfloat16)


def tail_rows(length, landing, width):
    lane = lax.broadcasted_iota(jnp.int32, (TAIL, width), 1)
    facts = jnp.where(lane == 0, length, jnp.where(lane == 1, landing, 0))
    return facts.astype(jnp.float32).astype(jnp.bfloat16)


def near_shapes(slots, width, heads, quarter):
    return [
        jax.ShapeDtypeStruct((slots * WINDOW, width), jnp.bfloat16),
        jax.ShapeDtypeStruct((slots * WINDOW, width), jnp.bfloat16),
        jax.ShapeDtypeStruct((slots * WINDOW, heads), jnp.float32),
        jax.ShapeDtypeStruct((slots * WINDOW, heads), jnp.bfloat16),
        jax.ShapeDtypeStruct((slots * TAIL, quarter), jnp.bfloat16),
    ]


def run_near_home(mp, table, tokens, shards, base, slots, w_out=None):
    heads = sum(w.shape[1] for w in shards) // 4
    width = tokens.shape[1]
    top = tokens.shape[0] // BLOCK - 1
    total_slots = table.shape[0] // 3
    more = [] if w_out is None else [w_out]
    extra = [] if w_out is None else [shards[0], w_out]

    def block_map(b, slot, table_ref):
        return (jnp.minimum(table_ref[total_slots + base + slot] + b, top), 0)

    local = pl.BlockSpec(memory_space=pltpu.VMEM)
    outs = pl.pallas_call(
        functools.partial(near_home_kernel, mp, len(shards), base, total_slots),
        grid_spec=pltpu.PrefetchScalarGridSpec(
            num_scalar_prefetch=1,
            grid=(slots,),
            in_specs=[
                pl.BlockSpec((BLOCK, width), functools.partial(block_map, b)) for b in range(MAXB)
            ]
            + [local] * (len(shards) + len(more)),
            out_specs=[local] * (5 + len(extra)),
        ),
        out_shape=near_shapes(slots, width, heads, width // mp)
        + [jax.ShapeDtypeStruct(a.shape, a.dtype) for a in extra],
        compiler_params=LIMIT,
        name="near_home",
    )(table, *([tokens] * MAXB), *shards, *more)
    outs = [in_vmem(out) for out in outs]
    return outs[:5], outs[5:]


def run_near_owner(mp, arrived, shards, slots):
    heads = sum(w.shape[1] for w in shards) // 4
    width = arrived.shape[1]
    local = pl.BlockSpec(memory_space=pltpu.VMEM)
    outs = pl.pallas_call(
        functools.partial(near_owner_kernel, len(shards)),
        grid=(slots,),
        in_specs=[local] * (1 + len(shards)),
        out_specs=[local] * 5,
        out_shape=near_shapes(slots, width, heads, width // mp),
        compiler_params=LIMIT,
        name="near_owner",
    )(in_vmem(arrived), *shards)
    return [in_vmem(out) for out in outs]


def run_far(mp, shards, near, w_perm, base, groups, paired, earlier=(), riders=()):
    width = w_perm.shape[1]
    quarter = width // mp
    joined = earlier[0].shape[0] // (WINDOW + TAIL) if earlier else 0
    size = (joined + groups) * (WINDOW + TAIL) + sum(r.shape[1] for r in riders) * TAIL
    local = pl.BlockSpec(memory_space=pltpu.VMEM)
    shapes = (
        [jax.ShapeDtypeStruct((2, size, quarter), jnp.bfloat16)] * (mp // 2)
        if paired
        else [jax.ShapeDtypeStruct((size, quarter), jnp.bfloat16)] * (0 if paired is None else mp)
    )
    states = [jax.ShapeDtypeStruct((mp, groups, TAIL, quarter), jnp.bfloat16)]
    states = [] if paired is False else states
    outs = pl.pallas_call(
        functools.partial(far_kernel, mp, len(shards), base, paired, joined, len(riders)),
        grid=(groups,),
        in_specs=[local] * (len(shards) + 6 + len(earlier) + len(riders)),
        out_specs=[local] * (len(shapes) + len(states)),
        scratch_shapes=[pltpu.VMEM((WINDOW + TAIL, width), jnp.float32)],
        out_shape=shapes + states,
        compiler_params=LIMIT,
        name="far_heads",
    )(*shards, *near, w_perm, *[in_vmem(a) for a in (*earlier, *riders)])
    return outs[: len(shapes)], outs[len(shapes) :]


def delta(mp, e, m):
    return e * mp + ((m >> 1) ^ ((m & 1) * (mp - 1)))


def plan_kernel(mp, per_pair, slots, ahead, *refs):
    len_ref, owner_ref, land_ref, start_ref, tokens_ref = refs[:5]
    home_ref, table_ref = refs[5:7]
    me, mine = lax.axis_index("dp"), lax.axis_index("mp")
    owners = home_ref.shape[0]
    users = len_ref.shape[1]
    chunk = -(-users // per_pair)
    top = tokens_ref.shape[0] // BLOCK - 1

    copies = []
    for i, (e, k) in enumerate(ahead):
        o = me ^ delta(mp, e, mine)
        length = start = landing = jnp.int32(0)
        for u in range(k * chunk, min((k + 1) * chunk, users)):
            hit = owner_ref[0, u] == o
            length = jnp.where(hit, len_ref[0, u], length)
            start = jnp.where(hit, start_ref[0, u], start)
            landing = jnp.where(hit, land_ref[0, u], landing)
        ahead_ref, sems = refs[7 + i], refs[-1]
        for b in range(MAXB):
            block = jnp.minimum(start + b, top)
            copies.append(
                pltpu.make_async_copy(
                    tokens_ref.at[pl.ds(pl.multiple_of(block * BLOCK, BLOCK), BLOCK), :],
                    ahead_ref.at[pl.ds(b * BLOCK, BLOCK), :],
                    sems.at[i * MAXB + b],
                )
            )
            copies[-1].start()
        ahead_ref[WINDOW:, :] = tail_rows(length, landing, tokens_ref.shape[1])

    def clear(o, c):
        for i in range(4 * per_pair):
            home_ref[o, i] = 0
        return c

    lax.fori_loop(0, owners, clear, 0)
    for u in range(users):
        k = u // chunk
        o = owner_ref[0, u]
        home_ref[o, 4 * k] = len_ref[0, u]
        home_ref[o, 4 * k + 1] = start_ref[0, u]
        home_ref[o, 4 * k + 2] = land_ref[0, u]
        home_ref[o, 4 * k + 3] = u
    for i, (e, k) in enumerate(slots):
        o = me ^ delta(mp, e, mine)
        for j in range(3):
            table_ref[j * len(slots) + i] = home_ref[o, 4 * k + j]
    for copy in copies:
        copy.wait()


def plan(dp, mp, per_pair, slots, ahead, tables, tokens):
    scalar = pl.BlockSpec(memory_space=pltpu.SMEM)
    local = pl.BlockSpec(memory_space=pltpu.VMEM)
    windows = [jax.ShapeDtypeStruct((WINDOW + TAIL, tokens.shape[1]), tokens.dtype)] * len(ahead)
    outs = pl.pallas_call(
        functools.partial(plan_kernel, mp, per_pair, slots, ahead),
        in_specs=[scalar] * len(tables) + [pl.BlockSpec(memory_space=pl.ANY)],
        out_specs=[scalar] * 2 + [local] * len(windows),
        out_shape=[
            jax.ShapeDtypeStruct((dp, 4 * per_pair), jnp.int32),
            jax.ShapeDtypeStruct((3 * len(slots),), jnp.int32),
        ]
        + windows,
        scratch_shapes=[pltpu.SemaphoreType.DMA((len(ahead) * MAXB,))] if ahead else [],
        compiler_params=LIMIT,
        name="plan_users",
    )(*tables, tokens)
    return outs[:2], outs[2:]


def place_kernel(mp, windows, states, count, home_ref, *refs):
    me, mine = lax.axis_index("dp"), lax.axis_index("mp")
    in_refs = refs[:count]
    out_ref, user_ref, users_ref, gather_ref, facts_ref, sem = refs[count:]
    windows = [
        (in_refs[array] if lead is None else in_refs[array].at[lead], first)
        for array, lead, first in windows
    ]
    for i, (ref, first) in enumerate(windows):
        row = first + WINDOW
        gather_ref[i : i + 1, :] = (
            ref[row : row + TAIL, :][0:1].astype(jnp.float32).astype(jnp.int32)
        )
    users_ref[...] = jnp.zeros_like(users_ref)
    for array, first, j, e, k in states:
        o = me ^ delta(mp, e, mine ^ j)

        @pl.when(home_ref[o, 4 * k] > 0)
        def _():
            users_ref[pl.ds(home_ref[o, 4 * k + 3], 1), :] = in_refs[array][
                first : first + TAIL, :
            ].astype(jnp.float32)[0:1]

    user_ref[...] = users_ref[...].astype(user_ref.dtype)
    copy = pltpu.make_async_copy(gather_ref, facts_ref, sem)
    copy.start()
    out_ref[...] = jnp.zeros_like(out_ref)
    copy.wait()
    for i, (ref, first) in enumerate(windows):
        for b in range(MAXB):

            @pl.when(facts_ref[i, 0] > b * BLOCK)
            def _():
                row = pl.multiple_of((facts_ref[i, 1] + b) * BLOCK, BLOCK)
                out_ref[pl.ds(row, BLOCK), :] = ref[first + b * BLOCK : first + (b + 1) * BLOCK, :]


def place(mp, windows, states, home, arrays, rows, users):
    quarter = arrays[0].shape[-1]
    local = pl.BlockSpec(memory_space=pltpu.VMEM)
    return pl.pallas_call(
        functools.partial(place_kernel, mp, windows, states, len(arrays)),
        in_specs=[pl.BlockSpec(memory_space=pltpu.SMEM)] + [local] * len(arrays),
        out_specs=[local, local],
        out_shape=[
            jax.ShapeDtypeStruct((rows, quarter), jnp.bfloat16),
            jax.ShapeDtypeStruct((users, quarter), jnp.bfloat16),
        ],
        scratch_shapes=[
            pltpu.VMEM((users, quarter), jnp.float32),
            pltpu.VMEM((len(windows), quarter), jnp.int32),
            pltpu.SMEM((len(windows), quarter), jnp.int32),
            pltpu.SemaphoreType.DMA(()),
        ],
        compiler_params=LIMIT,
        name="place_blocks",
    )(home, *[in_vmem(a) for a in arrays])


def per_device(dp, mp, tokens, w_uvqk, w_out, hist_len, owner, recv_offset, block_start):
    users = hist_len.shape[1]
    per_pair = -(-users // dp)
    rounds = dp // mp
    step = WINDOW + TAIL
    upper, lower = range(rounds // 2, rounds), range(rounds // 2)
    ahead = [(e, k) for e in upper for k in range(per_pair - 1)]
    late = [(e, per_pair - 1) for e in upper]
    local = [(e, k) for e in lower for k in range(per_pair)]
    slots = late + local

    def swap(value, j):
        return lax.ppermute(value, "mp", [(i, i ^ j) for i in range(mp)])

    def send(value, e, j):
        pairs = [
            (d * mp + m, (d ^ delta(mp, e, m)) * mp + (m ^ j)) for d in range(dp) for m in range(mp)
        ]
        return lax.ppermute(value, ("dp", "mp"), pairs)

    arrays, windows, states = [], [], []

    def arrive(array, count, lead=None):
        windows.extend((len(arrays), lead, i * step) for i in range(count))
        arrays.append(array)

    def relay(value, e, j):
        pairs = [
            (d * mp + m, (d ^ delta(mp, e, m ^ j)) * mp + m) for d in range(dp) for m in range(mp)
        ]
        return lax.ppermute(value, ("dp", "mp"), pairs)

    def cross(outs):
        crossed = []
        for p, out in enumerate(outs):
            crossed.append(swap(out, 2 * p) if p else out)
        return crossed

    def send_pairs(outs, jobs, crossed):
        pieces = []
        for e in sorted({e for e, _ in jobs}, reverse=True):
            turns = [i for i, (f, _) in enumerate(jobs) if f == e]
            rows = slice(turns[0] * step, (turns[-1] + 1) * step)
            for p, out in enumerate(outs):
                move = relay if crossed else send
                pieces.append((move(out[:, rows], e, 2 * p), len(turns)))
        return pieces

    def pass_on(pieces):
        for piece, count in pieces:
            arrive(piece, count, 0)
            arrive(swap(piece[1], 1), count)

    tokens = in_hbm(tokens)
    held = {0: w_uvqk}
    hop = mp // 2
    while hop >= 1:
        for shard, value in list(held.items()):
            held[shard + hop] = swap(value, hop)
        hop //= 2
    (home, table), windows_ahead = plan(
        dp,
        mp,
        per_pair,
        slots + ahead,
        ahead,
        [in_hbm(t) for t in (hist_len, owner, recv_offset, block_start)],
        tokens,
    )
    half = max(mp // 2, 1)
    sent = []
    for (e, _), window in zip(ahead, windows_ahead):
        sent.append(send(window, e, 0))
    near, (held[0], w_perm) = run_near_home(
        mp,
        table,
        tokens,
        [in_hbm(w_uvqk)] + [in_vmem(held[s]) for s in range(1, half)],
        0,
        len(slots),
        in_hbm(w_out),
    )
    shards = [in_vmem(held[s]) for s in range(mp)]
    late_outs, (late_state,) = run_far(
        mp, shards[half:], near, w_perm, 0, len(late), True
    )
    late_outs = cross(late_outs)
    outs, (local_state,) = run_far(mp, shards[half:], near, w_perm, len(late), len(local), True)
    local_pieces = send_pairs(outs, local, False)
    late_pieces = send_pairs(late_outs, late, True)
    parts = [late_state, local_state]
    order = slots
    if ahead:
        near = []
        for window in windows_ahead:
            near = run_near_owner(mp, window, shards[:half], 1)
            _, (part,) = run_far(mp, shards[half:], near, w_perm, 0, 1, None)
            parts.append(part)
        order = order + ahead
    earlier = ()
    for i in range(len(ahead)):
        near = run_near_owner(mp, sent[i], shards[:half], 1)
        riders = parts if i + 1 == len(ahead) else ()
        earlier, _ = run_far(mp, shards[half:], near, w_perm, 0, 1, False, earlier, riders)
    base = len(ahead) * step
    for j in range(mp):
        rows = earlier[j] if ahead else jnp.concatenate(
            [part[j].reshape(-1, part.shape[-1]) for part in parts], 0
        )
        states += [(len(arrays), base + i * TAIL, j, e, k) for i, (e, k) in enumerate(order)]
        arrive(swap(rows, j) if j else rows, len(ahead))
    pass_on(local_pieces)
    pass_on(late_pieces)
    return place(mp, windows, states, home, arrays, tokens.shape[0], users)


def solution(mesh):
    dp, mp = mesh.shape["dp"], mesh.shape["mp"]
    in_specs = (
        P("dp", None),
        P(None, "mp"),
        P(),
        P("dp", None),
        P("dp", None),
        P("dp", None),
        P("dp", None),
    )
    out_specs = (P("dp", "mp"), P("dp", "mp"))
    return jax.shard_map(
        functools.partial(per_device, dp, mp),
        mesh=mesh,
        in_specs=in_specs,
        out_specs=out_specs,
        check_vma=False,
    )
```

time: 82.4 us -> 80.6 us (0.978)
  waiting for transfers between devices: 39.1 us -> 30.7 us
  starting transfers between devices: 17.4 us -> 24.3 us
    ppermute x7 -> x4, waiting for transfers between devices: 32 us -> 8.1 us  [send(): return lax.ppermute(value, ('dp', 'mp'), pairs)]
    ppermute x9 -> x11, waiting for transfers between devices: 7.13 us -> 17.2 us  [swap(): return lax.ppermute(value, 'mp', [(i, i ^ j) for i in range(mp)])]
    ppermute x0 -> x2, waiting for transfers between devices: none -> 5.37 us  [relay(): return lax.ppermute(value, ('dp', 'mp'), pairs)]
    ppermute x0 -> x2, starting transfers between devices: none -> 5.34 us  [relay(): return lax.ppermute(value, ('dp', 'mp'), pairs)]
    ppermute x9 -> x11, starting transfers between devices: 9.22 us -> 12.6 us  [swap(): return lax.ppermute(value, 'mp', [(i, i ^ j) for i in range(mp)])]
    ppermute x7 -> x4, starting transfers between devices: 8.19 us -> 6.36 us  [send(): return lax.ppermute(value, ('dp', 'mp'), pairs)]
    pallas_call x1 -> x4, Pallas kernels: 2.41 us -> 3.49 us  [run_near_owner(): pl.pallas_call(functools.partial(near_owner_kernel, len(shards)), grid=(s...]
    pallas_call x1, Pallas kernels: 3.41 us -> 2.5 us  [plan(): pl.pallas_call(functools.partial(plan_kernel, mp, per_pair, slots, ahead)...]
  transfers between devices with their start and end apart: 16 -> 17, of which waited for: 7 -> 7; matrix products, arithmetic and copies ran while one was open for 0% -> 0% of each run, Pallas kernels for 22% -> 26%
where the time goes in v1:
time: 80.6 us; the launch traced here: 80.4 us
  waiting for transfers between devices  30.7 us (38%)
  Pallas kernels  24.6 us (31%)
  starting transfers between devices  24.3 us (30%)
    ppermute x11, waiting for transfers between devices, swap(): return lax.ppermute(value, 'mp', [(i, i ^ j) for i in range(mp)])  17.2 us
    ppermute x11, starting transfers between devices, swap(): return lax.ppermute(value, 'mp', [(i, i ^ j) for i in range(mp)])  12.6 us
    pallas_call x6, Pallas kernels, run_far(): pl.pallas_call(functools.partial(far_kernel, mp, len(shards), base, paire...  9.5 us
    ppermute x4, waiting for transfers between devices, send(): return lax.ppermute(value, ('dp', 'mp'), pairs)  8.1 us
    ppermute x4, starting transfers between devices, send(): return lax.ppermute(value, ('dp', 'mp'), pairs)  6.36 us
    pallas_call x1, Pallas kernels, run_near_home(): pl.pallas_call(functools.partial(near_home_kernel, mp, len(shards), base,...  5.78 us
    ppermute x2, waiting for transfers between devices, relay(): return lax.ppermute(value, ('dp', 'mp'), pairs)  5.37 us
    ppermute x2, starting transfers between devices, relay(): return lax.ppermute(value, ('dp', 'mp'), pairs)  5.34 us
  transfers between devices with their start and end apart: 17, of which 7 were waited for; matrix products, arithmetic and copies ran while one was open for 0% of the time, Pallas kernels for 26%

profile of v1, /device:TPU:0, one launch (start us, length us, event | category | flops | bytes accessed | tf_op | source)
XLA Modules:
  0.0 80.4 jit_solution(7673647923044220523)
XLA Ops:
  0.6 3.0 %collective-permute-start = (bf16[512,512]{1,0:T(8,128)(2,1)}, bf16[512,512]{1,0:T(8,128)(2,1)S(1)}, u32[]{:S(2)}, u32[]{:S(2)}) collective-permute-start(bf16[512,512]{1,0:T(8,128)(2,1)} %refs_2_.3), channel_id=1, source_target_pairs={{0,2},{1,3},{2,0},{3,1},{4,6},{5,7},{6,4},{7,5},{8,10},{9,11},{10,... | collective-permute-start | bytes 1572872 | tf_op jit(solution)/shard_map/ppermute | solution.py:432
  3.7 12.1 %collective-permute-done.refs_0_ = bf16[512,512]{1,0:T(8,128)(2,1)S(1)} collective-permute-done((bf16[512,512]{1,0:T(8,128)(2,1)}, bf16[512,512]{1,0:T(8,128)(2,1)S(1)}, u32[]{:S(2)}, u32[]{:S(2)}) %collective-permute-start) | collective-permute-done | bytes 524320 | tf_op jit(solution)/shard_map/ppermute | solution.py:432
  15.8 2.5 %plan_users.1 = (s32[8,12]{1,0:T(8,128)S(1)}, s32[18]{0:T(128)S(1)}, bf16[264,512]{1,0:T(8,128)(2,1)S(1)}, bf16[264,512]{1,0:T(8,128)(2,1)S(1)}) custom-call(s32[1,24]{1,0:T(1,128)} %refs_0_.2, s32[1,24]{1,0:T(1,128)} %refs_1_.2, s32[1,24]{1,0:T(1,128)} %refs_2_.2, s32[1,24]{1,0:T(1,128)} %refs_3_.1, bf16[6144,512]{1,0:T(8,128)(2,1)} %refs_1_.3), custom_call_target="tpu_custom_call" | custom-call | tf_op jit(solution)/shard_map/plan_users/pallas_call | solution.py:345
  18.3 2.9 %collective-permute-start.4 = (bf16[264,512]{1,0:T(8,128)(2,1)S(1)}, bf16[264,512]{1,0:T(8,128)(2,1)S(1)}, u32[]{:S(2)}, u32[]{:S(2)}) collective-permute-start(bf16[264,512]{1,0:T(8,128)(2,1)S(1)} %get-tuple-element.57.refs_0_), channel_id=1, source_target_pairs={{0,16},{1,29},{2,22},{3,27},{4,20},{5,25},{6,18},{7,31},{8,24},{9,... | collective-permute-start | bytes 811016 | tf_op jit(solution)/shard_map/ppermute | solution.py:438
  21.2 0.1 collective-permute-start.2
  21.3 5.8 %near_home.1 = (bf16[1024,512]{1,0:T(8,128)(2,1)S(1)}, bf16[1024,512]{1,0:T(8,128)(2,1)S(1)}, f32[1024,256]{1,0:T(8,128)S(1)}, bf16[1024,256]{1,0:T(8,128)(2,1)S...) custom-call(s32[18]{0:T(128)S(1)} %get-tuple-element.49.table_ref, ...), custom_call_target="tpu_custom_call" | custom-call | tf_op jit(solution)/shard_map/near_home/pallas_call | solution.py:223
  27.1 3.6 %far_heads.8 = (bf16[2,792,128]{2,1,0:T(8,128)(2,1)S(1)}, bf16[2,792,128]{2,1,0:T(8,128)(2,1)S(1)}, bf16[4,3,8,128]{3,2,1,0:T(8,128)(2,1)S(1)}) custom-call(bf16[512,512]{1,0:T(8,128)(2,1)S(1)} %collective-permute-done.refs_0_, bf16[512,512]{1,0:T(8,128)(2,1)S(1)} %collective-permute-done.1.refs_1_, bf16[1024,512]{1,0:T(8,128)(2,1)S(1)} %get-tuple-element.67.refs_2_, ...), custom_call_target="tpu_custom_call" | custom-call | tf_op jit(solution)/shard_map/far_heads/pallas_call | solution.py:272
  30.8 2.7 %collective-permute-start.10 = (bf16[2,792,128]{2,1,0:T(8,128)(2,1)S(1)}, bf16[2,792,128]{2,1,0:T(8,128)(2,1)S(1)}, u32[]{:S(2)}, u32[]{:S(2)}) collective-permute-start(bf16[2,792,128]{2,1,0:T(8,128)(2,1)S(1)} %get-tuple-element.89), channel_id=1, source_target_pairs={{0,2},{1,15},{2,4},{3,9},{4,6},{5,11},{6,0},{7,13},{8,10},{9,7},{1... | collective-permute-start | bytes 1216520 | tf_op jit(solution)/shard_map/ppermute | solution.py:438
  33.5 1.2 %far_heads.7 = (bf16[2,264,128]{2,1,0:T(8,128)(2,1)S(1)}, bf16[2,264,128]{2,1,0:T(8,128)(2,1)S(1)}, bf16[4,1,8,128]{3,2,1,0:T(8,128)(2,1)S(1)}) custom-call(bf16[512,512]{1,0:T(8,128)(2,1)S(1)} %collective-permute-done.refs_0_, bf16[512,512]{1,0:T(8,128)(2,1)S(1)} %collective-permute-done.1.refs_1_, bf16[1024,512]{1,0:T(8,128)(2,1)S(1)} %get-tuple-element.67.refs_2_, ...), custom_call_target="tpu_custom_call" | custom-call | tf_op jit(solution)/shard_map/far_heads/pallas_call | solution.py:272
  34.7 2.7 %collective-permute-start.12 = (bf16[2,264,128]{2,1,0:T(8,128)(2,1)S(1)}, bf16[2,264,128]{2,1,0:T(8,128)(2,1)S(1)}, u32[]{:S(2)}, u32[]{:S(2)}) collective-permute-start(bf16[2,264,128]{2,1,0:T(8,128)(2,1)S(1)} %get-tuple-element.90), channel_id=1, source_target_pairs={{0,16},{1,29},{2,22},{3,27},{4,20},{5,25},{6,18},{7,31},{8,24},{9,... | collective-permute-start | bytes 405512 | tf_op jit(solution)/shard_map/ppermute | solution.py:450
  37.3 0.9 %near_owner.7 = (bf16[256,512]{1,0:T(8,128)(2,1)S(1)}, bf16[256,512]{1,0:T(8,128)(2,1)S(1)}, f32[256,256]{1,0:T(8,128)S(1)}, bf16[256,256]{1,0:T(8,128)(2,1)S(1)}, bf16[8,128]{1,0:T(8,128)(2,1)S(1)}) custom-call(bf16[264,512]{1,0:T(8,128)(2,1)S(1)} %get-tuple-element.48.refs_0_, bf16[512,512]{1,0:T(8,128)(2,1)S(1)} %get-tuple-element.50.refs_1_, ...), custom_call_target="tpu_custom_call" | custom-call | tf_op jit(solution)/shard_map/near_owner/pallas_call | solution.py:247
  38.2 0.9 %near_owner.6 = (bf16[256,512]{1,0:T(8,128)(2,1)S(1)}, bf16[256,512]{1,0:T(8,128)(2,1)S(1)}, f32[256,256]{1,0:T(8,128)S(1)}, bf16[256,256]{1,0:T(8,128)(2,1)S(1)}, bf16[8,128]{1,0:T(8,128)(2,1)S(1)}) custom-call(bf16[264,512]{1,0:T(8,128)(2,1)S(1)} %get-tuple-element.57.refs_0_, bf16[512,512]{1,0:T(8,128)(2,1)S(1)} %get-tuple-element.50.refs_1_, ...), custom_call_target="tpu_custom_call" | custom-call | tf_op jit(solution)/shard_map/near_owner/pallas_call | solution.py:247
  39.1 0.3 collective-permute-done.4.refs_0_
  39.4 0.9 %near_owner.5 = (bf16[256,512]{1,0:T(8,128)(2,1)S(1)}, bf16[256,512]{1,0:T(8,128)(2,1)S(1)}, f32[256,256]{1,0:T(8,128)S(1)}, bf16[256,256]{1,0:T(8,128)(2,1)S(1)}, bf16[8,128]{1,0:T(8,128)(2,1)S(1)}) custom-call(bf16[264,512]{1,0:T(8,128)(2,1)S(1)} %collective-permute-done.4.refs_0_, bf16[512,512]{1,0:T(8,128)(2,1)S(1)} %get-tuple-element.50.refs_1_, ...), custom_call_target="tpu_custom_call" | custom-call | tf_op jit(solution)/shard_map/near_owner/pallas_call | solution.py:247
  40.2 7.8 %collective-permute-done.2.refs_0_ = bf16[264,512]{1,0:T(8,128)(2,1)S(1)} collective-permute-done((bf16[264,512]{1,0:T(8,128)(2,1)S(1)}, bf16[264,512]{1,0:T(8,128)(2,1)S(1)}, u32[]{:S(2)}, u32[]{:S(2)}) %collective-permute-start.2) | collective-permute-done | bytes 270368 | tf_op jit(solution)/shard_map/ppermute | solution.py:438
  48.1 0.9 %near_owner.4 = (bf16[256,512]{1,0:T(8,128)(2,1)S(1)}, bf16[256,512]{1,0:T(8,128)(2,1)S(1)}, f32[256,256]{1,0:T(8,128)S(1)}, bf16[256,256]{1,0:T(8,128)(2,1)S(1)}, bf16[8,128]{1,0:T(8,128)(2,1)S(1)}) custom-call(bf16[264,512]{1,0:T(8,128)(2,1)S(1)} %collective-permute-done.2.refs_0_, bf16[512,512]{1,0:T(8,128)(2,1)S(1)} %get-tuple-element.50.refs_1_, ...), custom_call_target="tpu_custom_call" | custom-call | tf_op jit(solution)/shard_map/near_owner/pallas_call | solution.py:247
  48.9 1.1 %far_heads.10.refs_15_ = bf16[4,1,8,128]{3,2,1,0:T(8,128)(2,1)S(1)} custom-call(bf16[512,512]{1,0:T(8,128)(2,1)S(1)} %collective-permute-done.refs_0_, bf16[512,512]{1,0:T(8,128)(2,1)S(1)} %collective-permute-done.1.refs_1_, bf16[256,512]{1,0:T(8,128)(2,1)S(1)} %get-tuple-element.79.refs_2_, bf16[256,512]{1,0:T(8,128)(2,1)S(1)} %get-tuple-element.80.refs_3_, ...), custom_call_target="tpu_custom_call" | custom-call | tf_op jit(solution)/shard_map/far_heads/pallas_call | solution.py:272
  50.0 1.1 %far_heads.9.refs_14_ = bf16[4,1,8,128]{3,2,1,0:T(8,128)(2,1)S(1)} custom-call(bf16[512,512]{1,0:T(8,128)(2,1)S(1)} %collective-permute-done.refs_0_, bf16[512,512]{1,0:T(8,128)(2,1)S(1)} %collective-permute-done.1.refs_1_, bf16[256,512]{1,0:T(8,128)(2,1)S(1)} %get-tuple-element.74.refs_2_, bf16[256,512]{1,0:T(8,128)(2,1)S(1)} %get-tuple-element.75.refs_3_, ...), custom_call_target="tpu_custom_call" | custom-call | tf_op jit(solution)/shard_map/far_heads/pallas_call | solution.py:272
  51.2 1.2 %far_heads.6 = (bf16[264,128]{1,0:T(8,128)(2,1)S(1)}, bf16[264,128]{1,0:T(8,128)(2,1)S(1)}, bf16[264,128]{1,0:T(8,128)(2,1)S(1)}, bf16[264,128]{1,0:T(8,128)(2,1)S(1)}) custom-call(bf16[512,512]{1,0:T(8,128)(2,1)S(1)} %collective-permute-done.refs_0_, bf16[512,512]{1,0:T(8,128)(2,1)S(1)} %collective-permute-done.1.refs_1_, ...), custom_call_target="tpu_custom_call" | custom-call | tf_op jit(solution)/shard_map/far_heads/pallas_call | solution.py:272
  52.4 1.2 %far_heads.11 = (bf16[576,128]{1,0:T(8,128)(2,1)S(1)}, bf16[576,128]{1,0:T(8,128)(2,1)S(1)}, bf16[576,128]{1,0:T(8,128)(2,1)S(1)}, bf16[576,128]{1,0:T(8,128)(2,1)S(1)}) custom-call(bf16[512,512]{1,0:T(8,128)(2,1)S(1)} %collective-permute-done.refs_0_, bf16[512,512]{1,0:T(8,128)(2,1)S(1)} %collective-permute-done.1.refs_1_, ...), custom_call_target="tpu_custom_call" | custom-call | tf_op jit(solution)/shard_map/far_heads/pallas_call | solution.py:272
  53.7 3.6 %collective-permute-start.6 = (bf16[576,128]{1,0:T(8,128)(2,1)S(1)}, bf16[576,128]{1,0:T(8,128)(2,1)S(1)}, u32[]{:S(2)}, u32[]{:S(2)}) collective-permute-start(bf16[576,128]{1,0:T(8,128)(2,1)S(1)} %get-tuple-element.86), channel_id=1, source_target_pairs={{0,2},{1,3},{2,0},{3,1},{4,6},{5,7},{6,4},{7,5},{8,10},{9,11},{10,... | collective-permute-start | bytes 442376 | tf_op jit(solution)/shard_map/ppermute | solution.py:432
  57.3 0.7 collective-permute-start.8
  57.9 2.5 %collective-permute-start.14 = (bf16[2,264,128]{2,1,0:T(8,128)(2,1)S(1)}, bf16[2,264,128]{2,1,0:T(8,128)(2,1)S(1)}, u32[]{:S(2)}, u32[]{:S(2)}) collective-permute-start(bf16[2,264,128]{2,1,0:T(8,128)(2,1)S(1)} %get-tuple-element.91), channel_id=1, source_target_pairs={{0,2},{1,3},{2,0},{3,1},{4,6},{5,7},{6,4},{7,5},{8,10},{9,11},{10,... | collective-permute-start | bytes 405512 | tf_op jit(solution)/shard_map/ppermute | solution.py:432
  60.4 3.9 %collective-permute-done.14 = bf16[2,264,128]{2,1,0:T(8,128)(2,1)S(1)} collective-permute-done((bf16[2,264,128]{2,1,0:T(8,128)(2,1)S(1)}, bf16[2,264,128]{2,1,0:T(8,128)(2,1)S(1)}, u32[]{:S(2)}, u32[]{:S(2)}) %collective-permute-start.14) | collective-permute-done | bytes 135200 | tf_op jit(solution)/shard_map/ppermute | solution.py:432
  64.3 1.2 %collective-permute-start.7 = (bf16[576,128]{1,0:T(8,128)(2,1)S(1)}, bf16[576,128]{1,0:T(8,128)(2,1)S(1)}, u32[]{:S(2)}, u32[]{:S(2)}) collective-permute-start(bf16[576,128]{1,0:T(8,128)(2,1)S(1)} %get-tuple-element.87), channel_id=1, source_target_pairs={{0,3},{1,2},{2,1},{3,0},{4,7},{5,6},{6,5},{7,4},{8,11},{9,10},{10,... | collective-permute-start | bytes 442376 | tf_op jit(solution)/shard_map/ppermute | solution.py:432
  65.5 2.7 %collective-permute-start.15 = (bf16[2,264,128]{2,1,0:T(8,128)(2,1)S(1)}, bf16[2,264,128]{2,1,0:T(8,128)(2,1)S(1)}, u32[]{:S(2)}, u32[]{:S(2)}) collective-permute-start(bf16[2,264,128]{2,1,0:T(8,128)(2,1)S(1)} %collective-permute-done.14), channel_id=1, source_target_pairs={{0,20},{1,25},{2,18},{3,31},{4,16},{5,29},{6,22},{7,27},{8,28},{9,... | collective-permute-start | bytes 405512 | tf_op jit(solution)/shard_map/ppermute | solution.py:450
  68.2 1.6 %collective-permute-start.11 = (bf16[792,128]{1,0:T(8,128)(2,1)S(1)}, bf16[792,128]{1,0:T(8,128)(2,1)S(1)}, u32[]{:S(2)}, u32[]{:S(2)}) collective-permute-start(bf16[792,128]{1,0:T(8,128)(2,1)S(1)} %slice_bitcast_fusion), channel_id=1, source_target_pairs={{0,1},{1,0},{2,3},{3,2},{4,5},{5,4},{6,7},{7,6},{8,9},{9,8},{10,11... | collective-permute-start | bytes 608264 | tf_op jit(solution)/shard_map/ppermute | solution.py:432
  69.9 5.4 %collective-permute-done.15.refs_10_ = bf16[2,264,128]{2,1,0:T(8,128)(2,1)S(1)} collective-permute-done((bf16[2,264,128]{2,1,0:T(8,128)(2,1)S(1)}, bf16[2,264,128]{2,1,0:T(8,128)(2,1)S(1)}, u32[]{:S(2)}, u32[]{:S(2)}) %collective-permute-start.15) | collective-permute-done | bytes 135200 | tf_op jit(solution)/shard_map/ppermute | solution.py:450
  75.3 0.6 collective-permute-start.13
  75.9 0.9 %collective-permute-done.13.refs_9_ = bf16[264,128]{1,0:T(8,128)(2,1)S(1)} collective-permute-done((bf16[264,128]{1,0:T(8,128)(2,1)S(1)}, bf16[264,128]{1,0:T(8,128)(2,1)S(1)}, u32[]{:S(2)}, u32[]{:S(2)}) %collective-permute-start.13) | collective-permute-done | bytes 67616 | tf_op jit(solution)/shard_map/ppermute | solution.py:432
  76.8 0.3 collective-permute-done.16.refs_11_
  77.1 3.3 %place_blocks.1 = (bf16[6144,128]{1,0:T(8,128)(2,1)}, bf16[24,128]{1,0:T(8,128)(2,1)}) custom-call(s32[8,12]{1,0:T(8,128)S(1)} %get-tuple-element.47.home_ref, bf16[576,128]{1,0:T(8,128)(2,1)S(1)} %get-tuple-element.84.refs_0_, bf16[576,128]{1,0:T(8,128)(2,1)S(1)} %collective-permute-done.5.refs_1_, bf16[576,128]{1,0:T(8,128)(2,1)S(1)} %collective-permute-done.6.refs_2_, ...), custom_call_target="tpu_custom_call" | custom-call | tf_op jit(solution)/shard_map/place_blocks/pallas_call | solution.py:401
  (19 shorter events, 0.2 us)
Async XLA Ops:
  0.6 15.2 %collective-permute-start = (bf16[512,512]{1,0:T(8,128)(2,1)}, bf16[512,512]{1,0:T(8,128)(2,1)S(1)}, u32[]{:S(2)}, u32[]{:S(2)}) collective-permute-start(bf16[512,512]{1,0:T(8,128)(2,1)} %refs_2_.3), channel_id=1, source_target_pairs={{0,2},{1,3},{2,0},{3,1},{4,6},{5,7},{6,4},{7,5},{8,10},{9,11},{10,... | collective-permute-start | bytes 1572872 | tf_op jit(solution)/shard_map/ppermute | solution.py:432
  3.7 17.6 %collective-permute-start.3 = (bf16[512,512]{1,0:T(8,128)(2,1)}, bf16[512,512]{1,0:T(8,128)(2,1)S(1)}, u32[]{:S(2)}, u32[]{:S(2)}) collective-permute-start(bf16[512,512]{1,0:T(8,128)(2,1)} %refs_2_.3), channel_id=1, source_target_pairs={{0,1},{1,0},{2,3},{3,2},{4,5},{5,4},{6,7},{7,6},{8,9},{9,8},{10,11... | collective-permute-start | bytes 1572872 | tf_op jit(solution)/shard_map/ppermute | solution.py:432
  15.8 11.3 %collective-permute-start.1 = (bf16[512,512]{1,0:T(8,128)(2,1)S(1)}, bf16[512,512]{1,0:T(8,128)(2,1)S(1)}, u32[]{:S(2)}, u32[]{:S(2)}) collective-permute-start(bf16[512,512]{1,0:T(8,128)(2,1)S(1)} %collective-permute-done.refs_0_), channel_id=1, source_target_pairs={{0,1},{1,0},{2,3},{3,2},{4,5},{5,4},{6,7},{7,6},{8,9},{9,8},{10,11... | collective-permute-start | bytes 1572872 | tf_op jit(solution)/shard_map/ppermute | solution.py:432
  18.3 21.1 %collective-permute-start.4 = (bf16[264,512]{1,0:T(8,128)(2,1)S(1)}, bf16[264,512]{1,0:T(8,128)(2,1)S(1)}, u32[]{:S(2)}, u32[]{:S(2)}) collective-permute-start(bf16[264,512]{1,0:T(8,128)(2,1)S(1)} %get-tuple-element.57.refs_0_), channel_id=1, source_target_pairs={{0,16},{1,29},{2,22},{3,27},{4,20},{5,25},{6,18},{7,31},{8,24},{9,... | collective-permute-start | bytes 811016 | tf_op jit(solution)/shard_map/ppermute | solution.py:438
  21.2 26.8 %collective-permute-start.2 = (bf16[264,512]{1,0:T(8,128)(2,1)S(1)}, bf16[264,512]{1,0:T(8,128)(2,1)S(1)}, u32[]{:S(2)}, u32[]{:S(2)}) collective-permute-start(bf16[264,512]{1,0:T(8,128)(2,1)S(1)} %get-tuple-element.48.refs_0_), channel_id=1, source_target_pairs={{0,16},{1,29},{2,22},{3,27},{4,20},{5,25},{6,18},{7,31},{8,24},{9,... | collective-permute-start | bytes 811016 | tf_op jit(solution)/shard_map/ppermute | solution.py:438
  30.8 34.8 %collective-permute-start.10 = (bf16[2,792,128]{2,1,0:T(8,128)(2,1)S(1)}, bf16[2,792,128]{2,1,0:T(8,128)(2,1)S(1)}, u32[]{:S(2)}, u32[]{:S(2)}) collective-permute-start(bf16[2,792,128]{2,1,0:T(8,128)(2,1)S(1)} %get-tuple-element.89), channel_id=1, source_target_pairs={{0,2},{1,15},{2,4},{3,9},{4,6},{5,11},{6,0},{7,13},{8,10},{9,7},{1... | collective-permute-start | bytes 1216520 | tf_op jit(solution)/shard_map/ppermute | solution.py:438
  34.7 23.3 %collective-permute-start.12 = (bf16[2,264,128]{2,1,0:T(8,128)(2,1)S(1)}, bf16[2,264,128]{2,1,0:T(8,128)(2,1)S(1)}, u32[]{:S(2)}, u32[]{:S(2)}) collective-permute-start(bf16[2,264,128]{2,1,0:T(8,128)(2,1)S(1)} %get-tuple-element.90), channel_id=1, source_target_pairs={{0,16},{1,29},{2,22},{3,27},{4,20},{5,25},{6,18},{7,31},{8,24},{9,... | collective-permute-start | bytes 405512 | tf_op jit(solution)/shard_map/ppermute | solution.py:450
  53.6 21.6 %collective-permute-start.5 = (bf16[576,128]{1,0:T(8,128)(2,1)S(1)}, bf16[576,128]{1,0:T(8,128)(2,1)S(1)}, u32[]{:S(2)}, u32[]{:S(2)}) collective-permute-start(bf16[576,128]{1,0:T(8,128)(2,1)S(1)} %get-tuple-element.85), channel_id=1, source_target_pairs={{0,1},{1,0},{2,3},{3,2},{4,5},{5,4},{6,7},{7,6},{8,9},{9,8},{10,11... | collective-permute-start | bytes 442376 | tf_op jit(solution)/shard_map/ppermute | solution.py:432
  53.7 22.1 %collective-permute-start.6 = (bf16[576,128]{1,0:T(8,128)(2,1)S(1)}, bf16[576,128]{1,0:T(8,128)(2,1)S(1)}, u32[]{:S(2)}, u32[]{:S(2)}) collective-permute-start(bf16[576,128]{1,0:T(8,128)(2,1)S(1)} %get-tuple-element.86), channel_id=1, source_target_pairs={{0,2},{1,3},{2,0},{3,1},{4,6},{5,7},{6,4},{7,5},{8,10},{9,11},{10,... | collective-permute-start | bytes 442376 | tf_op jit(solution)/shard_map/ppermute | solution.py:432
  57.3 11.0 %collective-permute-start.8 = (bf16[2,792,128]{2,1,0:T(8,128)(2,1)S(1)}, bf16[2,792,128]{2,1,0:T(8,128)(2,1)S(1)}, u32[]{:S(2)}, u32[]{:S(2)}) collective-permute-start(bf16[2,792,128]{2,1,0:T(8,128)(2,1)S(1)} %get-tuple-element.88), channel_id=1, source_target_pairs={{0,0},{1,13},{2,6},{3,11},{4,4},{5,9},{6,2},{7,15},{8,8},{9,5},{10... | collective-permute-start | bytes 1216520 | tf_op jit(solution)/shard_map/ppermute | solution.py:438
  57.9 6.4 %collective-permute-start.14 = (bf16[2,264,128]{2,1,0:T(8,128)(2,1)S(1)}, bf16[2,264,128]{2,1,0:T(8,128)(2,1)S(1)}, u32[]{:S(2)}, u32[]{:S(2)}) collective-permute-start(bf16[2,264,128]{2,1,0:T(8,128)(2,1)S(1)} %get-tuple-element.91), channel_id=1, source_target_pairs={{0,2},{1,3},{2,0},{3,1},{4,6},{5,7},{6,4},{7,5},{8,10},{9,11},{10,... | collective-permute-start | bytes 405512 | tf_op jit(solution)/shard_map/ppermute | solution.py:432
  64.3 11.6 %collective-permute-start.7 = (bf16[576,128]{1,0:T(8,128)(2,1)S(1)}, bf16[576,128]{1,0:T(8,128)(2,1)S(1)}, u32[]{:S(2)}, u32[]{:S(2)}) collective-permute-start(bf16[576,128]{1,0:T(8,128)(2,1)S(1)} %get-tuple-element.87), channel_id=1, source_target_pairs={{0,3},{1,2},{2,1},{3,0},{4,7},{5,6},{6,5},{7,4},{8,11},{9,10},{10,... | collective-permute-start | bytes 442376 | tf_op jit(solution)/shard_map/ppermute | solution.py:432
  65.5 9.7 %collective-permute-start.15 = (bf16[2,264,128]{2,1,0:T(8,128)(2,1)S(1)}, bf16[2,264,128]{2,1,0:T(8,128)(2,1)S(1)}, u32[]{:S(2)}, u32[]{:S(2)}) collective-permute-start(bf16[2,264,128]{2,1,0:T(8,128)(2,1)S(1)} %collective-permute-done.14), channel_id=1, source_target_pairs={{0,20},{1,25},{2,18},{3,31},{4,16},{5,29},{6,22},{7,27},{8,28},{9,... | collective-permute-start | bytes 405512 | tf_op jit(solution)/shard_map/ppermute | solution.py:450
  68.2 8.9 %collective-permute-start.11 = (bf16[792,128]{1,0:T(8,128)(2,1)S(1)}, bf16[792,128]{1,0:T(8,128)(2,1)S(1)}, u32[]{:S(2)}, u32[]{:S(2)}) collective-permute-start(bf16[792,128]{1,0:T(8,128)(2,1)S(1)} %slice_bitcast_fusion), channel_id=1, source_target_pairs={{0,1},{1,0},{2,3},{3,2},{4,5},{5,4},{6,7},{7,6},{8,9},{9,8},{10,11... | collective-permute-start | bytes 608264 | tf_op jit(solution)/shard_map/ppermute | solution.py:432
  75.2 1.9 %collective-permute-start.9 = (bf16[792,128]{1,0:T(8,128)(2,1)S(1)}, bf16[792,128]{1,0:T(8,128)(2,1)S(1)}, u32[]{:S(2)}, u32[]{:S(2)}) collective-permute-start(bf16[792,128]{1,0:T(8,128)(2,1)S(1)} %slice_bitcast_fusion.1), channel_id=1, source_target_pairs={{0,1},{1,0},{2,3},{3,2},{4,5},{5,4},{6,7},{7,6},{8,9},{9,8},{10,11... | collective-permute-start | bytes 608264 | tf_op jit(solution)/shard_map/ppermute | solution.py:432
  75.3 1.5 %collective-permute-start.13 = (bf16[264,128]{1,0:T(8,128)(2,1)S(1)}, bf16[264,128]{1,0:T(8,128)(2,1)S(1)}, u32[]{:S(2)}, u32[]{:S(2)}) collective-permute-start(bf16[264,128]{1,0:T(8,128)(2,1)S(1)} %slice_bitcast_fusion.3), channel_id=1, source_target_pairs={{0,1},{1,0},{2,3},{3,2},{4,5},{5,4},{6,7},{7,6},{8,9},{9,8},{10,11... | collective-permute-start | bytes 202760 | tf_op jit(solution)/shard_map/ppermute | solution.py:432
  75.8 1.3 %collective-permute-start.16 = (bf16[264,128]{1,0:T(8,128)(2,1)S(1)}, bf16[264,128]{1,0:T(8,128)(2,1)S(1)}, u32[]{:S(2)}, u32[]{:S(2)}) collective-permute-start(bf16[264,128]{1,0:T(8,128)(2,1)S(1)} %slice_bitcast_fusion.2), channel_id=1, source_target_pairs={{0,1},{1,0},{2,3},{3,2},{4,5},{5,4},{6,7},{7,6},{8,9},{9,8},{10,11... | collective-permute-start | bytes 202760 | tf_op jit(solution)/shard_map/ppermute | solution.py:432

commit v2 on v1

--- a/solution.py
+++ b/solution.py
@@ -111,23 +111,13 @@
     near_rows(slot, widened, w_refs, near_refs[:-1])
 
 
-def near_owner_kernel(near, *refs):
-    arrived_ref, w_refs = refs[0], refs[1 : 1 + near]
-    tail_ref = refs[-1]
-    slot = pl.program_id(0)
-    first = pl.multiple_of(slot * (WINDOW + TAIL), TAIL)
-    tail_ref[pl.ds(pl.multiple_of(slot * TAIL, TAIL), TAIL), :] = arrived_ref[
-        pl.ds(first + WINDOW, TAIL), : tail_ref.shape[1]
-    ]
-    near_rows(slot, arrived_ref[pl.ds(first, WINDOW), :].astype(jnp.float32), w_refs, refs[1 + near : -1])
-
-
-def far_kernel(mp, far, base, paired, joined, riders, *refs):
+def far_kernel(mp, far, base, fused, paired, joined, riders, *refs):
     w_refs = refs[:far]
-    rows_ref, half_ref, near_value_ref, near_gate_ref, tail_ref, wp_ref = refs[far : far + 6]
+    taken = far + (2 if fused else 6)
+    near_refs, wp_ref = refs[far : taken - 1], refs[taken - 1]
     stated = paired is not False
-    earlier = refs[far + 6 : far + 6 + (mp if joined else 0)]
-    taken = far + 6 + len(earlier)
+    earlier = refs[taken : taken + (mp if joined else 0)]
+    taken += len(earlier)
     rider_refs = refs[taken : taken + riders]
     out_refs = refs[taken + riders : -2]
     state_ref, mixed_ref = refs[-2:]
@@ -146,12 +136,21 @@
     slot = pl.program_id(0)
     mine = lax.axis_index("mp")
     width = wp_ref.shape[0]
-    rows = pl.ds(pl.multiple_of((base + slot) * WINDOW, WINDOW), WINDOW)
-    tail = tail_ref[pl.ds(pl.multiple_of((base + slot) * TAIL, TAIL), TAIL), :]
+    if fused:
+        (window_ref,) = near_refs
+        tail = window_ref[WINDOW:, : width // mp]
+        widened = window_ref[:WINDOW, :].astype(jnp.float32)
+        values, gates = attend_heads(norm_half(widened), w_refs)
+        value, gate = jnp.concatenate(values, 1), jnp.concatenate(gates, 1)
+    else:
+        rows_ref, half_ref, near_value_ref, near_gate_ref, tail_ref = near_refs
+        rows = pl.ds(pl.multiple_of((base + slot) * WINDOW, WINDOW), WINDOW)
+        tail = tail_ref[pl.ds(pl.multiple_of((base + slot) * TAIL, TAIL), TAIL), :]
+        widened = rows_ref[rows, :].astype(jnp.float32)
+        values, gates = attend_heads(half_ref[rows, :], w_refs)
+        value = jnp.concatenate([near_value_ref[rows, :]] + values, 1)
+        gate = jnp.concatenate([near_gate_ref[rows, :]] + gates, 1)
     length = tail.astype(jnp.float32)[0:1, 0:1]
-    values, gates = attend_heads(half_ref[rows, :], w_refs)
-    value = jnp.concatenate([near_value_ref[rows, :]] + values, 1)
-    gate = jnp.concatenate([near_gate_ref[rows, :]] + gates, 1)
     average, scale = norm_scale(
         jnp.sum(value, 1, keepdims=True) * (1.0 / WINDOW),
         jnp.sum(value * value, 1, keepdims=True) * (1.0 / WINDOW**2),
@@ -159,7 +158,6 @@
     )
     average, scale = average * WINDOW, scale * (1.0 / WINDOW)
     gated = (value - average) * scale * gate.astype(jnp.float32)
-    widened = rows_ref[rows, :].astype(jnp.float32)
     live = lax.broadcasted_iota(jnp.int32, (WINDOW, 1), 0).astype(jnp.float32)
     final = live == length - 1.0
     quarter = width // mp
@@ -240,22 +238,6 @@
     return outs[:5], outs[5:]
 
 
-def run_near_owner(mp, arrived, shards, slots):
-    heads = sum(w.shape[1] for w in shards) // 4
-    width = arrived.shape[1]
-    local = pl.BlockSpec(memory_space=pltpu.VMEM)
-    outs = pl.pallas_call(
-        functools.partial(near_owner_kernel, len(shards)),
-        grid=(slots,),
-        in_specs=[local] * (1 + len(shards)),
-        out_specs=[local] * 5,
-        out_shape=near_shapes(slots, width, heads, width // mp),
-        compiler_params=LIMIT,
-        name="near_owner",
-    )(in_vmem(arrived), *shards)
-    return [in_vmem(out) for out in outs]
-
-
 def run_far(mp, shards, near, w_perm, base, groups, paired, earlier=(), riders=()):
     width = w_perm.shape[1]
     quarter = width // mp
@@ -270,9 +252,9 @@
     states = [jax.ShapeDtypeStruct((mp, groups, TAIL, quarter), jnp.bfloat16)]
     states = [] if paired is False else states
     outs = pl.pallas_call(
-        functools.partial(far_kernel, mp, len(shards), base, paired, joined, len(riders)),
+        functools.partial(far_kernel, mp, len(shards), base, len(near) == 1, paired, joined, len(riders)),
         grid=(groups,),
-        in_specs=[local] * (len(shards) + 6 + len(earlier) + len(riders)),
+        in_specs=[local] * (len(shards) + len(near) + 1 + len(earlier) + len(riders)),
         out_specs=[local] * (len(shapes) + len(states)),
         scratch_shapes=[pltpu.VMEM((WINDOW + TAIL, width), jnp.float32)],
         out_shape=shapes + states,
@@ -361,7 +343,8 @@
 def place_kernel(mp, windows, states, count, home_ref, *refs):
     me, mine = lax.axis_index("dp"), lax.axis_index("mp")
     in_refs = refs[:count]
-    out_ref, user_ref, users_ref, gather_ref, facts_ref, sem = refs[count:]
+    out_ref, user_ref, users_ref, gather_ref, facts_ref, taken_ref, zero_ref, rounded_ref, sems = refs[count:]
+    blocks = out_ref.shape[0] // BLOCK
     windows = [
         (in_refs[array] if lead is None else in_refs[array].at[lead], first)
         for array, lead, first in windows
@@ -371,6 +354,11 @@
         gather_ref[i : i + 1, :] = (
             ref[row : row + TAIL, :][0:1].astype(jnp.float32).astype(jnp.int32)
         )
+    facts = pltpu.make_async_copy(gather_ref, facts_ref, sems.at[0])
+    zero_ref[...] = jnp.zeros_like(zero_ref)
+    for i in range(blocks):
+        taken_ref[i] = 0
+    facts.start()
     users_ref[...] = jnp.zeros_like(users_ref)
     for array, first, j, e, k in states:
         o = me ^ delta(mp, e, mine ^ j)
@@ -381,18 +369,39 @@
                 first : first + TAIL, :
             ].astype(jnp.float32)[0:1]
 
-    user_ref[...] = users_ref[...].astype(user_ref.dtype)
-    copy = pltpu.make_async_copy(gather_ref, facts_ref, sem)
-    copy.start()
-    out_ref[...] = jnp.zeros_like(out_ref)
-    copy.wait()
+    rounded_ref[...] = users_ref[...].astype(user_ref.dtype)
+    state_copy = pltpu.make_async_copy(rounded_ref, user_ref, sems.at[2])
+    state_copy.start()
+    facts.wait()
     for i, (ref, first) in enumerate(windows):
+        length, block = facts_ref[i, 0], facts_ref[i, 1]
         for b in range(MAXB):
 
-            @pl.when(facts_ref[i, 0] > b * BLOCK)
+            @pl.when((length > b * BLOCK) & (length <= (b + 1) * BLOCK))
             def _():
-                row = pl.multiple_of((facts_ref[i, 1] + b) * BLOCK, BLOCK)
-                out_ref[pl.ds(row, BLOCK), :] = ref[first + b * BLOCK : first + (b + 1) * BLOCK, :]
+                for c in range(b + 1):
+                    taken_ref[block + c] = 1
+                size = (b + 1) * BLOCK
+                pltpu.make_async_copy(
+                    ref.at[pl.ds(first, size), :],
+                    out_ref.at[pl.ds(pl.multiple_of(block * BLOCK, BLOCK), size), :],
+                    sems.at[1],
+                ).start()
+
+    def fill(i, c):
+        @pl.when(taken_ref[i] == 0)
+        def _():
+            pltpu.make_async_copy(
+                zero_ref,
+                out_ref.at[pl.ds(pl.multiple_of(i * BLOCK, BLOCK), BLOCK), :],
+                sems.at[1],
+            ).start()
+
+        return c
+
+    lax.fori_loop(0, blocks, fill, 0)
+    pltpu.make_async_copy(out_ref, out_ref, sems.at[1]).wait()
+    state_copy.wait()
 
 
 def place(mp, windows, states, home, arrays, rows, users):
@@ -401,7 +410,7 @@
     return pl.pallas_call(
         functools.partial(place_kernel, mp, windows, states, len(arrays)),
         in_specs=[pl.BlockSpec(memory_space=pltpu.SMEM)] + [local] * len(arrays),
-        out_specs=[local, local],
+        out_specs=[pl.BlockSpec(memory_space=pl.ANY)] * 2,
         out_shape=[
             jax.ShapeDtypeStruct((rows, quarter), jnp.bfloat16),
             jax.ShapeDtypeStruct((users, quarter), jnp.bfloat16),
@@ -410,7 +419,10 @@
             pltpu.VMEM((users, quarter), jnp.float32),
             pltpu.VMEM((len(windows), quarter), jnp.int32),
             pltpu.SMEM((len(windows), quarter), jnp.int32),
-            pltpu.SemaphoreType.DMA(()),
+            pltpu.SMEM((rows // BLOCK,), jnp.int32),
+            pltpu.VMEM((BLOCK, quarter), jnp.bfloat16),
+            pltpu.VMEM((users, quarter), jnp.bfloat16),
+            pltpu.SemaphoreType.DMA((3,)),
         ],
         compiler_params=LIMIT,
         name="place_blocks",
@@ -510,17 +522,16 @@
     parts = [late_state, local_state]
     order = slots
     if ahead:
-        near = []
         for window in windows_ahead:
-            near = run_near_owner(mp, window, shards[:half], 1)
-            _, (part,) = run_far(mp, shards[half:], near, w_perm, 0, 1, None)
+            _, (part,) = run_far(
+                mp, shards, [in_vmem(window)], w_perm, 0, 1, None
+            )
             parts.append(part)
         order = order + ahead
     earlier = ()
     for i in range(len(ahead)):
-        near = run_near_owner(mp, sent[i], shards[:half], 1)
         riders = parts if i + 1 == len(ahead) else ()
-        earlier, _ = run_far(mp, shards[half:], near, w_perm, 0, 1, False, earlier, riders)
+        earlier, _ = run_far(mp, shards, [in_vmem(sent[i])], w_perm, 0, 1, False, earlier, riders)
     base = len(ahead) * step
     for j in range(mp):
         rows = earlier[j] if ahead else jnp.concatenate(

time: 80.6 us -> 73.4 us (0.911)
  waiting for transfers between devices: 30.7 us -> 26 us
  Pallas kernels: 24.6 us -> 21.8 us
    ppermute x2, waiting for transfers between devices: 5.37 us -> 0.01 us  [relay(): return lax.ppermute(value, ('dp', 'mp'), pairs)]
    ppermute x4, waiting for transfers between devices: 8.1 us -> 13 us  [send(): return lax.ppermute(value, ('dp', 'mp'), pairs)]
    ppermute x11, waiting for transfers between devices: 17.2 us -> 13.1 us  [swap(): return lax.ppermute(value, 'mp', [(i, i ^ j) for i in range(mp)])]
    pallas_call x10 -> x6, Pallas kernels: 13 us -> 11 us  [run_far(): pl.pallas_call(functools.partial(far_kernel, mp, len(shards), base, len(n...]
    ppermute x4, starting transfers between devices: 6.36 us -> 4.53 us  [send(): return lax.ppermute(value, ('dp', 'mp'), pairs)]
    ppermute x2, starting transfers between devices: 5.34 us -> 7.11 us  [relay(): return lax.ppermute(value, ('dp', 'mp'), pairs)]
  transfers between devices with their start and end apart: 17 -> 17, of which waited for: 7 -> 5; matrix products, arithmetic and copies ran while one was open for 0% -> 0% of each run, Pallas kernels for 26% -> 26%
where the time goes in v2:
time: 73.4 us; the launch traced here: 73.2 us
  waiting for transfers between devices  26 us (35%)
  starting transfers between devices  24.6 us (34%)
  Pallas kernels  21.8 us (30%)
  between operations  0.76 us (1%)
    ppermute x11, waiting for transfers between devices, swap(): return lax.ppermute(value, 'mp', [(i, i ^ j) for i in range(mp)])  13.1 us
    ppermute x11, starting transfers between devices, swap(): return lax.ppermute(value, 'mp', [(i, i ^ j) for i in range(mp)])  13 us
    ppermute x4, waiting for transfers between devices, send(): return lax.ppermute(value, ('dp', 'mp'), pairs)  13 us
    pallas_call x6, Pallas kernels, run_far(): pl.pallas_call(functools.partial(far_kernel, mp, len(shards), base, len(n...  11 us
    ppermute x2, starting transfers between devices, relay(): return lax.ppermute(value, ('dp', 'mp'), pairs)  7.11 us
    pallas_call x1, Pallas kernels, run_near_home(): pl.pallas_call(functools.partial(near_home_kernel, mp, len(shards), base,...  5.78 us
    ppermute x4, starting transfers between devices, send(): return lax.ppermute(value, ('dp', 'mp'), pairs)  4.53 us
    pallas_call x1, Pallas kernels, place(): pl.pallas_call(functools.partial(place_kernel, mp, windows, states, len(a...  2.51 us
  transfers between devices with their start and end apart: 17, of which 5 were waited for; matrix products, arithmetic and copies ran while one was open for 0% of the time, Pallas kernels for 26%

profile of v2, /device:TPU:0, one launch (start us, length us, event | category | flops | bytes accessed | tf_op | source)
XLA Modules:
  0.0 73.2 jit_solution(10647941861792000654)
XLA Ops:
  0.6 3.0 %collective-permute-start.1 = (bf16[512,512]{1,0:T(8,128)(2,1)}, bf16[512,512]{1,0:T(8,128)(2,1)S(1)}, u32[]{:S(2)}, u32[]{:S(2)}) collective-permute-start(bf16[512,512]{1,0:T(8,128)(2,1)} %refs_2_.3), channel_id=1, source_target_pairs={{0,2},{1,3},{2,0},{3,1},{4,6},{5,7},{6,4},{7,5},{8,10},{9,11},{10,... | collective-permute-start | bytes 1572872 | tf_op jit(solution)/shard_map/ppermute | solution.py:444
  3.7 0.0 collective-permute-start
  3.7 12.1 %collective-permute-done.1.refs_2_.refs_0_ = bf16[512,512]{1,0:T(8,128)(2,1)S(1)} collective-permute-done((bf16[512,512]{1,0:T(8,128)(2,1)}, bf16[512,512]{1,0:T(8,128)(2,1)S(1)}, u32[]{:S(2)}, u32[]{:S(2)}) %collective-permute-start.1) | collective-permute-done | bytes 524320 | tf_op jit(solution)/shard_map/ppermute | solution.py:444
  15.8 2.5 %plan_users.1 = (s32[8,12]{1,0:T(8,128)S(1)}, s32[18]{0:T(128)S(1)}, bf16[264,512]{1,0:T(8,128)(2,1)S(1)}, bf16[264,512]{1,0:T(8,128)(2,1)S(1)}) custom-call(s32[1,24]{1,0:T(1,128)} %refs_0_.2, s32[1,24]{1,0:T(1,128)} %refs_1_.2, s32[1,24]{1,0:T(1,128)} %refs_2_.2, s32[1,24]{1,0:T(1,128)} %refs_3_.1, bf16[6144,512]{1,0:T(8,128)(2,1)} %refs_1_.3), custom_call_target="tpu_custom_call" | custom-call | tf_op jit(solution)/shard_map/plan_users/pallas_call | solution.py:327
  18.3 2.9 %collective-permute-start.4 = (bf16[264,512]{1,0:T(8,128)(2,1)S(1)}, bf16[264,512]{1,0:T(8,128)(2,1)S(1)}, u32[]{:S(2)}, u32[]{:S(2)}) collective-permute-start(bf16[264,512]{1,0:T(8,128)(2,1)S(1)} %get-tuple-element.32.refs_4_), channel_id=1, source_target_pairs={{0,16},{1,29},{2,22},{3,27},{4,20},{5,25},{6,18},{7,31},{8,24},{9,... | collective-permute-start | bytes 811016 | tf_op jit(solution)/shard_map/ppermute | solution.py:450
  21.2 0.1 collective-permute-start.3
  21.3 5.8 %near_home.1 = (bf16[1024,512]{1,0:T(8,128)(2,1)S(1)}, bf16[1024,512]{1,0:T(8,128)(2,1)S(1)}, f32[1024,256]{1,0:T(8,128)S(1)}, bf16[1024,256]{1,0:T(8,128)(2,1)S...) custom-call(s32[18]{0:T(128)S(1)} %get-tuple-element.28.table_ref, ...), custom_call_target="tpu_custom_call" | custom-call | tf_op jit(solution)/shard_map/near_home/pallas_call | solution.py:221
  27.1 0.0 collective-permute-done.2.refs_3_.refs_1_
  27.1 3.6 %far_heads.8 = (bf16[2,792,128]{2,1,0:T(8,128)(2,1)S(1)}, bf16[2,792,128]{2,1,0:T(8,128)(2,1)S(1)}, bf16[4,3,8,128]{3,2,1,0:T(8,128)(2,1)S(1)}) custom-call(bf16[512,512]{1,0:T(8,128)(2,1)S(1)} %collective-permute-done.1.refs_2_.refs_0_, bf16[512,512]{1,0:T(8,128)(2,1)S(1)} %collective-permute-done.2.refs_3_.refs_1_, ...), custom_call_target="tpu_custom_call" | custom-call | tf_op jit(solution)/shard_map/far_heads/pallas_call | solution.py:254
  30.8 0.7 collective-permute-start.8
  31.5 1.2 %far_heads.7 = (bf16[2,264,128]{2,1,0:T(8,128)(2,1)S(1)}, bf16[2,264,128]{2,1,0:T(8,128)(2,1)S(1)}, bf16[4,1,8,128]{3,2,1,0:T(8,128)(2,1)S(1)}) custom-call(bf16[512,512]{1,0:T(8,128)(2,1)S(1)} %collective-permute-done.1.refs_2_.refs_0_, bf16[512,512]{1,0:T(8,128)(2,1)S(1)} %collective-permute-done.2.refs_3_.refs_1_, ...), custom_call_target="tpu_custom_call" | custom-call | tf_op jit(solution)/shard_map/far_heads/pallas_call | solution.py:254
  32.7 2.9 %collective-permute-start.12 = (bf16[2,264,128]{2,1,0:T(8,128)(2,1)S(1)}, bf16[2,264,128]{2,1,0:T(8,128)(2,1)S(1)}, u32[]{:S(2)}, u32[]{:S(2)}) collective-permute-start(bf16[2,264,128]{2,1,0:T(8,128)(2,1)S(1)} %get-tuple-element.50), channel_id=1, source_target_pairs={{0,16},{1,29},{2,22},{3,27},{4,20},{5,25},{6,18},{7,31},{8,24},{9,... | collective-permute-start | bytes 405512 | tf_op jit(solution)/shard_map/ppermute | solution.py:462
  35.6 5.1 %collective-permute-start.14 = (bf16[2,264,128]{2,1,0:T(8,128)(2,1)S(1)}, bf16[2,264,128]{2,1,0:T(8,128)(2,1)S(1)}, u32[]{:S(2)}, u32[]{:S(2)}) collective-permute-start(bf16[2,264,128]{2,1,0:T(8,128)(2,1)S(1)} %get-tuple-element.51), channel_id=1, source_target_pairs={{0,2},{1,3},{2,0},{3,1},{4,6},{5,7},{6,4},{7,5},{8,10},{9,11},{10,... | collective-permute-start | bytes 405512 | tf_op jit(solution)/shard_map/ppermute | solution.py:444
  40.7 1.5 %far_heads.10.refs_13_ = bf16[4,1,8,128]{3,2,1,0:T(8,128)(2,1)S(1)} custom-call(bf16[512,512]{1,0:T(8,128)(2,1)S(1)} %get-tuple-element.29.refs_0_, bf16[512,512]{1,0:T(8,128)(2,1)S(1)} %collective-permute-done.refs_3_.refs_1_, bf16[512,512]{1,0:T(8,128)(2,1)S(1)} %collective-permute-done.1.refs_2_.refs_0_, ...), custom_call_target="tpu_custom_call" | custom-call | tf_op jit(solution)/shard_map/far_heads/pallas_call | solution.py:254
  42.1 1.5 %far_heads.9.refs_12_ = bf16[4,1,8,128]{3,2,1,0:T(8,128)(2,1)S(1)} custom-call(bf16[512,512]{1,0:T(8,128)(2,1)S(1)} %get-tuple-element.29.refs_0_, bf16[512,512]{1,0:T(8,128)(2,1)S(1)} %collective-permute-done.refs_3_.refs_1_, bf16[512,512]{1,0:T(8,128)(2,1)S(1)} %collective-permute-done.1.refs_2_.refs_0_, ...), custom_call_target="tpu_custom_call" | custom-call | tf_op jit(solution)/shard_map/far_heads/pallas_call | solution.py:254
  43.6 0.0 collective-permute-done.4.refs_4_
  43.6 1.6 %far_heads.6 = (bf16[264,128]{1,0:T(8,128)(2,1)S(1)}, bf16[264,128]{1,0:T(8,128)(2,1)S(1)}, bf16[264,128]{1,0:T(8,128)(2,1)S(1)}, bf16[264,128]{1,0:T(8,128)(2,1)S(1)}) custom-call(bf16[512,512]{1,0:T(8,128)(2,1)S(1)} %get-tuple-element.29.refs_0_, bf16[512,512]{1,0:T(8,128)(2,1)S(1)} %collective-permute-done.refs_3_.refs_1_, ...), custom_call_target="tpu_custom_call" | custom-call | tf_op jit(solution)/shard_map/far_heads/pallas_call | solution.py:254
  45.2 2.8 %collective-permute-done.3.refs_4_ = bf16[264,512]{1,0:T(8,128)(2,1)S(1)} collective-permute-done((bf16[264,512]{1,0:T(8,128)(2,1)S(1)}, bf16[264,512]{1,0:T(8,128)(2,1)S(1)}, u32[]{:S(2)}, u32[]{:S(2)}) %collective-permute-start.3) | collective-permute-done | bytes 270368 | tf_op jit(solution)/shard_map/ppermute | solution.py:450
  48.1 1.6 %far_heads.11 = (bf16[576,128]{1,0:T(8,128)(2,1)S(1)}, bf16[576,128]{1,0:T(8,128)(2,1)S(1)}, bf16[576,128]{1,0:T(8,128)(2,1)S(1)}, bf16[576,128]{1,0:T(8,128)(2,1)S(1)}) custom-call(bf16[512,512]{1,0:T(8,128)(2,1)S(1)} %get-tuple-element.29.refs_0_, bf16[512,512]{1,0:T(8,128)(2,1)S(1)} %collective-permute-done.refs_3_.refs_1_, ...), custom_call_target="tpu_custom_call" | custom-call | tf_op jit(solution)/shard_map/far_heads/pallas_call | solution.py:254
  49.7 0.1 collective-permute-start.5
  49.7 3.6 %collective-permute-start.6 = (bf16[576,128]{1,0:T(8,128)(2,1)S(1)}, bf16[576,128]{1,0:T(8,128)(2,1)S(1)}, u32[]{:S(2)}, u32[]{:S(2)}) collective-permute-start(bf16[576,128]{1,0:T(8,128)(2,1)S(1)} %get-tuple-element.46), channel_id=1, source_target_pairs={{0,2},{1,3},{2,0},{3,1},{4,6},{5,7},{6,4},{7,5},{8,10},{9,11},{10,... | collective-permute-start | bytes 442376 | tf_op jit(solution)/shard_map/ppermute | solution.py:444
  53.3 0.9 %collective-permute-start.10 = (bf16[2,792,128]{2,1,0:T(8,128)(2,1)S(1)}, bf16[2,792,128]{2,1,0:T(8,128)(2,1)S(1)}, u32[]{:S(2)}, u32[]{:S(2)}) collective-permute-start(bf16[2,792,128]{2,1,0:T(8,128)(2,1)S(1)} %get-tuple-element.49), channel_id=1, source_target_pairs={{0,2},{1,15},{2,4},{3,9},{4,6},{5,11},{6,0},{7,13},{8,10},{9,7},{1... | collective-permute-start | bytes 1216520 | tf_op jit(solution)/shard_map/ppermute | solution.py:450
  54.2 0.1 collective-permute-start.7
  54.3 4.2 %collective-permute-start.15 = (bf16[2,264,128]{2,1,0:T(8,128)(2,1)S(1)}, bf16[2,264,128]{2,1,0:T(8,128)(2,1)S(1)}, u32[]{:S(2)}, u32[]{:S(2)}) collective-permute-start(bf16[2,264,128]{2,1,0:T(8,128)(2,1)S(1)} %collective-permute-done.14), channel_id=1, source_target_pairs={{0,20},{1,25},{2,18},{3,31},{4,16},{5,29},{6,22},{7,27},{8,28},{9,... | collective-permute-start | bytes 405512 | tf_op jit(solution)/shard_map/ppermute | solution.py:462
  58.5 10.1 %collective-permute-done.10.refs_6_ = bf16[2,792,128]{2,1,0:T(8,128)(2,1)S(1)} collective-permute-done((bf16[2,792,128]{2,1,0:T(8,128)(2,1)S(1)}, bf16[2,792,128]{2,1,0:T(8,128)(2,1)S(1)}, u32[]{:S(2)}, u32[]{:S(2)}) %collective-permute-start.10) | collective-permute-done | bytes 405536 | tf_op jit(solution)/shard_map/ppermute | solution.py:450
  68.6 0.0 collective-permute-start.9
  68.6 0.6 collective-permute-start.11
  69.2 0.1 collective-permute-start.13
  69.3 0.5 collective-permute-start.16
  69.8 0.7 %collective-permute-done.13.refs_9_ = bf16[264,128]{1,0:T(8,128)(2,1)S(1)} collective-permute-done((bf16[264,128]{1,0:T(8,128)(2,1)S(1)}, bf16[264,128]{1,0:T(8,128)(2,1)S(1)}, u32[]{:S(2)}, u32[]{:S(2)}) %collective-permute-start.13) | collective-permute-done | bytes 67616 | tf_op jit(solution)/shard_map/ppermute | solution.py:444
  70.5 0.2 collective-permute-done.16.refs_11_
  70.7 2.5 %place_blocks.1 = (bf16[6144,128]{1,0:T(8,128)(2,1)}, bf16[24,128]{1,0:T(8,128)(2,1)}) custom-call(s32[8,12]{1,0:T(8,128)S(1)} %get-tuple-element.27.home_ref, bf16[576,128]{1,0:T(8,128)(2,1)S(1)} %get-tuple-element.44.refs_0_, bf16[576,128]{1,0:T(8,128)(2,1)S(1)} %collective-permute-done.5.refs_1_, bf16[576,128]{1,0:T(8,128)(2,1)S(1)} %collective-permute-done.6.refs_2_, ...), custom_call_target="tpu_custom_call" | custom-call | tf_op jit(solution)/shard_map/place_blocks/pallas_call | solution.py:410
  (15 shorter events, 0.1 us)
Async XLA Ops:
  0.6 15.2 %collective-permute-start.1 = (bf16[512,512]{1,0:T(8,128)(2,1)}, bf16[512,512]{1,0:T(8,128)(2,1)S(1)}, u32[]{:S(2)}, u32[]{:S(2)}) collective-permute-start(bf16[512,512]{1,0:T(8,128)(2,1)} %refs_2_.3), channel_id=1, source_target_pairs={{0,2},{1,3},{2,0},{3,1},{4,6},{5,7},{6,4},{7,5},{8,10},{9,11},{10,... | collective-permute-start | bytes 1572872 | tf_op jit(solution)/shard_map/ppermute | solution.py:444
  3.7 17.6 %collective-permute-start = (bf16[512,512]{1,0:T(8,128)(2,1)}, bf16[512,512]{1,0:T(8,128)(2,1)S(1)}, u32[]{:S(2)}, u32[]{:S(2)}) collective-permute-start(bf16[512,512]{1,0:T(8,128)(2,1)} %refs_2_.3), channel_id=1, source_target_pairs={{0,1},{1,0},{2,3},{3,2},{4,5},{5,4},{6,7},{7,6},{8,9},{9,8},{10,11... | collective-permute-start | bytes 1572872 | tf_op jit(solution)/shard_map/ppermute | solution.py:444
  15.8 11.3 %collective-permute-start.2 = (bf16[512,512]{1,0:T(8,128)(2,1)S(1)}, bf16[512,512]{1,0:T(8,128)(2,1)S(1)}, u32[]{:S(2)}, u32[]{:S(2)}) collective-permute-start(bf16[512,512]{1,0:T(8,128)(2,1)S(1)} %collective-permute-done.1.refs_2_.refs_0_), channel_id=1, source_target_pairs={{0,1},{1,0},{2,3},{3,2},{4,5},{5,4},{6,7},{7,6},{8,9},{9,8},{10,11... | collective-permute-start | bytes 1572872 | tf_op jit(solution)/shard_map/ppermute | solution.py:444
  18.3 25.3 %collective-permute-start.4 = (bf16[264,512]{1,0:T(8,128)(2,1)S(1)}, bf16[264,512]{1,0:T(8,128)(2,1)S(1)}, u32[]{:S(2)}, u32[]{:S(2)}) collective-permute-start(bf16[264,512]{1,0:T(8,128)(2,1)S(1)} %get-tuple-element.32.refs_4_), channel_id=1, source_target_pairs={{0,16},{1,29},{2,22},{3,27},{4,20},{5,25},{6,18},{7,31},{8,24},{9,... | collective-permute-start | bytes 811016 | tf_op jit(solution)/shard_map/ppermute | solution.py:450
  21.2 26.8 %collective-permute-start.3 = (bf16[264,512]{1,0:T(8,128)(2,1)S(1)}, bf16[264,512]{1,0:T(8,128)(2,1)S(1)}, u32[]{:S(2)}, u32[]{:S(2)}) collective-permute-start(bf16[264,512]{1,0:T(8,128)(2,1)S(1)} %get-tuple-element.30.refs_4_), channel_id=1, source_target_pairs={{0,16},{1,29},{2,22},{3,27},{4,20},{5,25},{6,18},{7,31},{8,24},{9,... | collective-permute-start | bytes 811016 | tf_op jit(solution)/shard_map/ppermute | solution.py:450
  30.8 23.5 %collective-permute-start.8 = (bf16[2,792,128]{2,1,0:T(8,128)(2,1)S(1)}, bf16[2,792,128]{2,1,0:T(8,128)(2,1)S(1)}, u32[]{:S(2)}, u32[]{:S(2)}) collective-permute-start(bf16[2,792,128]{2,1,0:T(8,128)(2,1)S(1)} %get-tuple-element.48), channel_id=1, source_target_pairs={{0,0},{1,13},{2,6},{3,11},{4,4},{5,9},{6,2},{7,15},{8,8},{9,5},{10... | collective-permute-start | bytes 1216520 | tf_op jit(solution)/shard_map/ppermute | solution.py:450
  32.7 20.6 %collective-permute-start.12 = (bf16[2,264,128]{2,1,0:T(8,128)(2,1)S(1)}, bf16[2,264,128]{2,1,0:T(8,128)(2,1)S(1)}, u32[]{:S(2)}, u32[]{:S(2)}) collective-permute-start(bf16[2,264,128]{2,1,0:T(8,128)(2,1)S(1)} %get-tuple-element.50), channel_id=1, source_target_pairs={{0,16},{1,29},{2,22},{3,27},{4,20},{5,25},{6,18},{7,31},{8,24},{9,... | collective-permute-start | bytes 405512 | tf_op jit(solution)/shard_map/ppermute | solution.py:462
  35.6 18.6 %collective-permute-start.14 = (bf16[2,264,128]{2,1,0:T(8,128)(2,1)S(1)}, bf16[2,264,128]{2,1,0:T(8,128)(2,1)S(1)}, u32[]{:S(2)}, u32[]{:S(2)}) collective-permute-start(bf16[2,264,128]{2,1,0:T(8,128)(2,1)S(1)} %get-tuple-element.51), channel_id=1, source_target_pairs={{0,2},{1,3},{2,0},{3,1},{4,6},{5,7},{6,4},{7,5},{8,10},{9,11},{10,... | collective-permute-start | bytes 405512 | tf_op jit(solution)/shard_map/ppermute | solution.py:444
  49.7 19.6 %collective-permute-start.5 = (bf16[576,128]{1,0:T(8,128)(2,1)S(1)}, bf16[576,128]{1,0:T(8,128)(2,1)S(1)}, u32[]{:S(2)}, u32[]{:S(2)}) collective-permute-start(bf16[576,128]{1,0:T(8,128)(2,1)S(1)} %get-tuple-element.45), channel_id=1, source_target_pairs={{0,1},{1,0},{2,3},{3,2},{4,5},{5,4},{6,7},{7,6},{8,9},{9,8},{10,11... | collective-permute-start | bytes 442376 | tf_op jit(solution)/shard_map/ppermute | solution.py:444
  49.7 19.6 %collective-permute-start.6 = (bf16[576,128]{1,0:T(8,128)(2,1)S(1)}, bf16[576,128]{1,0:T(8,128)(2,1)S(1)}, u32[]{:S(2)}, u32[]{:S(2)}) collective-permute-start(bf16[576,128]{1,0:T(8,128)(2,1)S(1)} %get-tuple-element.46), channel_id=1, source_target_pairs={{0,2},{1,3},{2,0},{3,1},{4,6},{5,7},{6,4},{7,5},{8,10},{9,11},{10,... | collective-permute-start | bytes 442376 | tf_op jit(solution)/shard_map/ppermute | solution.py:444
  53.3 15.3 %collective-permute-start.10 = (bf16[2,792,128]{2,1,0:T(8,128)(2,1)S(1)}, bf16[2,792,128]{2,1,0:T(8,128)(2,1)S(1)}, u32[]{:S(2)}, u32[]{:S(2)}) collective-permute-start(bf16[2,792,128]{2,1,0:T(8,128)(2,1)S(1)} %get-tuple-element.49), channel_id=1, source_target_pairs={{0,2},{1,15},{2,4},{3,9},{4,6},{5,11},{6,0},{7,13},{8,10},{9,7},{1... | collective-permute-start | bytes 1216520 | tf_op jit(solution)/shard_map/ppermute | solution.py:450
  54.2 15.6 %collective-permute-start.7 = (bf16[576,128]{1,0:T(8,128)(2,1)S(1)}, bf16[576,128]{1,0:T(8,128)(2,1)S(1)}, u32[]{:S(2)}, u32[]{:S(2)}) collective-permute-start(bf16[576,128]{1,0:T(8,128)(2,1)S(1)} %get-tuple-element.47), channel_id=1, source_target_pairs={{0,3},{1,2},{2,1},{3,0},{4,7},{5,6},{6,5},{7,4},{8,11},{9,10},{10,... | collective-permute-start | bytes 442376 | tf_op jit(solution)/shard_map/ppermute | solution.py:444
  54.3 14.4 %collective-permute-start.15 = (bf16[2,264,128]{2,1,0:T(8,128)(2,1)S(1)}, bf16[2,264,128]{2,1,0:T(8,128)(2,1)S(1)}, u32[]{:S(2)}, u32[]{:S(2)}) collective-permute-start(bf16[2,264,128]{2,1,0:T(8,128)(2,1)S(1)} %collective-permute-done.14), channel_id=1, source_target_pairs={{0,20},{1,25},{2,18},{3,31},{4,16},{5,29},{6,22},{7,27},{8,28},{9,... | collective-permute-start | bytes 405512 | tf_op jit(solution)/shard_map/ppermute | solution.py:462
  68.6 2.1 %collective-permute-start.9 = (bf16[792,128]{1,0:T(8,128)(2,1)S(1)}, bf16[792,128]{1,0:T(8,128)(2,1)S(1)}, u32[]{:S(2)}, u32[]{:S(2)}) collective-permute-start(bf16[792,128]{1,0:T(8,128)(2,1)S(1)} %slice_bitcast_fusion.1), channel_id=1, source_target_pairs={{0,1},{1,0},{2,3},{3,2},{4,5},{5,4},{6,7},{7,6},{8,9},{9,8},{10,11... | collective-permute-start | bytes 608264 | tf_op jit(solution)/shard_map/ppermute | solution.py:444
  68.6 2.1 %collective-permute-start.11 = (bf16[792,128]{1,0:T(8,128)(2,1)S(1)}, bf16[792,128]{1,0:T(8,128)(2,1)S(1)}, u32[]{:S(2)}, u32[]{:S(2)}) collective-permute-start(bf16[792,128]{1,0:T(8,128)(2,1)S(1)} %slice_bitcast_fusion), channel_id=1, source_target_pairs={{0,1},{1,0},{2,3},{3,2},{4,5},{5,4},{6,7},{7,6},{8,9},{9,8},{10,11... | collective-permute-start | bytes 608264 | tf_op jit(solution)/shard_map/ppermute | solution.py:444
  69.2 1.3 %collective-permute-start.13 = (bf16[264,128]{1,0:T(8,128)(2,1)S(1)}, bf16[264,128]{1,0:T(8,128)(2,1)S(1)}, u32[]{:S(2)}, u32[]{:S(2)}) collective-permute-start(bf16[264,128]{1,0:T(8,128)(2,1)S(1)} %slice_bitcast_fusion.3), channel_id=1, source_target_pairs={{0,1},{1,0},{2,3},{3,2},{4,5},{5,4},{6,7},{7,6},{8,9},{9,8},{10,11... | collective-permute-start | bytes 202760 | tf_op jit(solution)/shard_map/ppermute | solution.py:444
  69.3 1.4 %collective-permute-start.16 = (bf16[264,128]{1,0:T(8,128)(2,1)S(1)}, bf16[264,128]{1,0:T(8,128)(2,1)S(1)}, u32[]{:S(2)}, u32[]{:S(2)}) collective-permute-start(bf16[264,128]{1,0:T(8,128)(2,1)S(1)} %slice_bitcast_fusion.2), channel_id=1, source_target_pairs={{0,1},{1,0},{2,3},{3,2},{4,5},{5,4},{6,7},{7,6},{8,9},{9,8},{10,11... | collective-permute-start | bytes 202760 | tf_op jit(solution)/shard_map/ppermute | solution.py:444
